TPU v7x, 128 devices: a whole 4x4x4 slice. The times are simulated.
128 devices in a mesh: gx: 4 (over z_lo, core), gy: 16 (over x, y), gz: 2 (over z_hi).
Axes of the slice: x: 4, y: 4, z: 4 (z_hi: 2, z_lo: 2; z = z_hi * 2 + z_lo), core: 2. Of those that a mesh axis runs over, the one named last changes fastest.
Arguments:
- eigvecs: bfloat16 [64, 128, 96, 512], P('gx', 'gy', 'gz'), may hold values from -7 to 7, as said below
- material: float32 [2, 64, 128, 96], P(None, 'gx', 'gy', 'gz'), may hold values from 0.5 to 2
Outputs:
- stiffness: float32 [512, 512], P(('gx', 'gy', 'gz'))
- mass_matrix: float32 [512, 512], P(('gx', 'gy', 'gz'))
Inputs may be any that keep to these rules, and one draw needn't show every extreme that they name: `eigvecs`: entries are a rough part plus a part that varies slowly over the grid.
All inputs are finite; a program needn't handle non-finite values.
Results may differ from a plain program's by a relative error of at most 0.0003.
Values may be sent and summed in bfloat16 or wider, within the bound.
A program may use at most 128 MiB of HBM per device.

v0:
```python
import jax
import jax.numpy as jnp
from jax import lax
from jax.sharding import PartitionSpec as P

corner_weight = 0.0625
coupling_total = 3.5
mass_side = 1.0 / 6.0
mass_middle = 4.0 / 6.0


def with_halo(cells, sides, width):
    for axis, dim in sides:
        count = lax.axis_size(axis)
        ends = count - 1
        head = lax.slice_in_dim(cells, 0, width, axis=dim)
        tail = lax.slice_in_dim(cells, cells.shape[dim] - width, cells.shape[dim], axis=dim)
        cells = jnp.concatenate(
            [
                lax.ppermute(tail, axis, [(i, (i + 1) % count) for i in range(ends)]),
                cells,
                lax.ppermute(head, axis, [((i + 1) % count, i) for i in range(ends)]),
            ],
            axis=dim,
        )
    return cells


def split_up(x, dim, devices):
    dims = x.shape
    parts = x.reshape(*dims[:dim], devices, dims[dim] // devices, *dims[dim + 1 :])
    return jnp.moveaxis(parts, dim, 0)


def sum_at_owner(x, axis, dim):
    devices = lax.axis_size(axis)
    parts = lax.all_to_all(split_up(x, dim, devices), axis, 0, 0, tiled=True)
    return jnp.sum(parts, axis=0)


def three_taps(field, side, middle):
    for axis_dim in (0, 1, 2):
        inner = field.shape[axis_dim] - 2
        lower = lax.slice_in_dim(field, 0, inner, axis=axis_dim)
        centre = lax.slice_in_dim(field, 1, inner + 1, axis=axis_dim)
        upper = lax.slice_in_dim(field, 2, inner + 2, axis=axis_dim)
        field = side * (lower + upper) + middle * centre
    return field


def apply_operators(padded, padded_material):
    values = padded.astype(jnp.float32)
    kappa = padded_material[0]
    rho = padded_material[1]
    centre = values[1:-1, 1:-1, 1:-1]
    kappa_centre = kappa[1:-1, 1:-1, 1:-1]
    rho_centre = rho[1:-1, 1:-1, 1:-1]
    kappa_values = kappa[..., None] * values
    rho_values = rho[..., None] * values
    self_weight = 8.0 * corner_weight
    near_values = corner_weight * three_taps(values, 1.0, 2.0) - self_weight * centre
    near_kappa_values = (
        corner_weight * three_taps(kappa_values, 1.0, 2.0)
        - self_weight * kappa_values[1:-1, 1:-1, 1:-1]
    )
    near_kappa = corner_weight * three_taps(kappa, 1.0, 2.0) - self_weight * kappa_centre
    row_weight = 0.5 * (coupling_total * kappa_centre + near_kappa)
    stiff_sum = (
        row_weight[..., None] * centre
        - 0.5 * kappa_centre[..., None] * near_values
        - 0.5 * near_kappa_values
    )
    mass_sum = 0.5 * rho_centre[..., None] * three_taps(
        values, mass_side, mass_middle
    ) + 0.5 * three_taps(rho_values, mass_side, mass_middle)
    return (stiff_sum.astype(jnp.bfloat16), mass_sum.astype(jnp.bfloat16))


def per_device(eigvecs, material):
    size_x, size_y, size_z, columns = eigvecs.shape
    cells = size_x * size_y * size_z
    block_cols = 128
    padded_material = with_halo(material, (("gx", 1), ("gy", 2), ("gz", 3)), 1)
    padded = with_halo(eigvecs, (("gx", 0), ("gy", 1), ("gz", 2)), 1)

    def column_block(block_index):
        col_block = lax.dynamic_slice_in_dim(padded, block_index * block_cols, block_cols, 3)
        stiff_vecs, mass_vecs = apply_operators(col_block, padded_material)
        return (stiff_vecs.reshape(cells, block_cols), mass_vecs.reshape(cells, block_cols))

    stiff_blocks, mass_blocks = lax.map(
        column_block, jnp.arange(columns // block_cols, dtype=jnp.int32)
    )
    flat_vectors = eigvecs.reshape(cells, columns)
    devices_all = lax.axis_size("gx") * lax.axis_size("gy") * lax.axis_size("gz")
    total_cells = cells * devices_all
    row_count = columns // lax.axis_size("gx") * lax.axis_size("gx")
    stiff_part = jnp.einsum(
        "cp,bcq->pbq", flat_vectors, stiff_blocks, preferred_element_type=jnp.float32
    ).reshape(row_count, columns)
    mass_part = jnp.einsum(
        "cp,bcq->pbq", flat_vectors, mass_blocks, preferred_element_type=jnp.float32
    ).reshape(row_count, columns)
    section_one = sum_at_owner(jnp.concatenate([stiff_part, mass_part], axis=1), "gx", 0)
    section_two = sum_at_owner(section_one, "gy", 0)
    summed = sum_at_owner(section_two, "gz", 0)
    stiffness = summed[:, :columns] / total_cells
    mass_matrix = summed[:, columns:] / total_cells
    return (stiffness, mass_matrix)


def solution(mesh):
    return jax.shard_map(
        per_device,
        mesh=mesh,
        in_specs=(P("gx", "gy", "gz", None), P(None, "gx", "gy", "gz")),
        out_specs=(P(("gx", "gy", "gz"), None), P(("gx", "gy", "gz"), None)),
        check_vma=False,
    )
```

profile of v0, /device:TPU:0, one launch (start us, length us, event | category | flops | bytes accessed | tf_op | source)
XLA Modules:
  0.0 277.3 jit_solution(3379979988916823563)
XLA Ops:
  3.8 4.6 %collective-permute-start = (f32[2,1,8,48]{3,2,1,0:T(8,128)S(1)}, f32[2,1,8,48]{3,2,1,0:T(8,128)S(1)}, u32[]{:S(2)}, u32[]{:S(2)}) collective-permute-start(f32[2,1,8,48]{3,2,1,0:T(8,128)S(1)} %get-tuple-element.101), channel_id=1, source_target_pairs={{0,32},{32,64},{64,96},{1,33},{33,65},{65,97},{2,34},{34,66},{66,9... | collective-permute-start | bytes 9224 | tf_op jit(solution)/shard_map/ppermute | solution.py:20
  11.2 3.9 %constant_dynamic-update-slice_fusion.6 = bf16[18,8,48,512]{3,2,1,0:T(8,128)(2,1)S(1)} fusion(bf16[18,8,48,512]{3,2,1,0:T(8,128)(2,1)S(1)} %constant_dynamic-update-slice_fusion.7, bf16[16,8,48,512]{3,2,1,0:T(8,128)(2,1)} %param.4), kind=kLoop, calls=%fused_computation.87 | loop fusion | bytes 12582912
  20.7 5.5 %collective-permute-start.8 = (bf16[18,1,48,512]{3,2,1,0:T(8,128)(2,1)}, bf16[18,1,48,512]{3,2,1,0:T(8,128)(2,1)}, u32[]{:S(2)}, u32[]{:S(2)}) collective-permute-start(bf16[18,1,48,512]{3,2,1,0:T(8,128)(2,1)} %get-tuple-element.92), channel_id=1, source_target_pairs={{0,2},{2,4},{4,6},{6,8},{8,10},{10,12},{12,14},{14,16},{16,18},{18... | collective-permute-start | bytes 2654216 | tf_op jit(solution)/shard_map/ppermute | solution.py:20
  27.8 4.5 %collective-permute-start.2 = (f32[2,18,1,48]{3,2,1,0:T(1,128)S(1)}, f32[2,18,1,48]{3,2,1,0:T(1,128)S(1)}, u32[]{:S(2)}, u32[]{:S(2)}) collective-permute-start(f32[2,18,1,48]{3,2,1,0:T(1,128)S(1)} %get-tuple-element.98), channel_id=1, source_target_pairs={{0,2},{2,4},{4,6},{6,8},{8,10},{10,12},{12,14},{14,16},{16,18},{18... | collective-permute-start | bytes 20744 | tf_op jit(solution)/shard_map/ppermute | solution.py:20
  32.3 8.1 %collective-permute-done.3 = f32[2,18,1,48]{3,2,1,0:T(1,128)S(1)} collective-permute-done((f32[2,18,1,48]{3,2,1,0:T(1,128)S(1)}, f32[2,18,1,48]{3,2,1,0:T(1,128)S(1)}, u32[]{:S(2)}, u32[]{:S(2)}) %collective-permute-start.3) | collective-permute-done | bytes 6944 | tf_op jit(solution)/shard_map/ppermute | solution.py:22
  44.5 6.8 %collective-permute-start.4 = (f32[2,18,10,1]{3,2,1,0:T(8,128)}, f32[2,18,10,1]{3,2,1,0:T(8,128)}, u32[]{:S(2)}, u32[]{:S(2)}) collective-permute-start(f32[2,18,10,1]{3,2,1,0:T(8,128)} %get-tuple-element.96), channel_id=1, source_target_pairs={{0,1},{2,3},{4,5},{6,7},{8,9},{10,11},{12,13},{14,15},{16,17},{18,... | collective-permute-start | bytes 4328 | tf_op jit(solution)/shard_map/ppermute | solution.py:20
  60.9 6.3 %collective-permute-start.10 = (bf16[18,10,1,512]{3,2,1,0:T(2,128)(2,1)S(1)}, bf16[18,10,1,512]{3,2,1,0:T(2,128)(2,1)S(1)}, u32[]{:S(2)}, u32[]{:S(2)}) collective-permute-start(bf16[18,10,1,512]{3,2,1,0:T(2,128)(2,1)S(1)} %get-tuple-element.90), channel_id=1, source_target_pairs={{0,1},{2,3},{4,5},{6,7},{8,9},{10,11},{12,13},{14,15},{16,17},{18,... | collective-permute-start | bytes 552968 | tf_op jit(solution)/shard_map/ppermute | solution.py:20
  67.2 5.5 %collective-permute-done.11 = bf16[18,10,1,512]{3,2,1,0:T(2,128)(2,1)S(1)} collective-permute-done((bf16[18,10,1,512]{3,2,1,0:T(2,128)(2,1)S(1)}, bf16[18,10,1,512]{3,2,1,0:T(2,128)(2,1)S(1)}, u32[]{:S(2)}, u32[]{:S(2)}) %collective-permute-start.11) | collective-permute-done | bytes 184352 | tf_op jit(solution)/shard_map/ppermute | solution.py:22
  74.5 9.4 %pad_maximum_fusion = bf16[18,10,50,512]{3,2,1,0:T(8,128)(2,1)} fusion(bf16[18,10,1,512]{3,2,1,0:T(2,128)(2,1)S(1)} %collective-permute-done.11, bf16[18,1,48,512]{3,2,1,0:T(8,128)(2,1)} %collective-permute-done.9, bf16[18,8,48,512]{3,2,1,0:T(8,128)(2,1)S(1)} %bitcast.42, bf16[18,1,48,512]{3,2,1,0:T(8,128)(2,1)} %collective-permute-done.8, ...), kind=kLoop, calls=%fused_computation.72 | loop fusion | flops 46080000 | bytes 18432000 | tf_op jit(solution)/shard_map/concatenate | solution.py:18
  83.9 114.4 %while.13 = (s32[]{:T(128)}, bf16[4,6144,128]{2,1,0:T(8,128)(2,1)}, bf16[4,6144,128]{2,1,0:T(8,128)(2,1)}, f32[2,18,10,50]{3,2,1,0:T(8,128)S(1)}, f32[16,10,50]{...) while((s32[]{:T(128)}, bf16[4,6144,128]{2,1,0:T(8,128)(2,1)}, ...), condition=%wide.region_1.2_spmd, body=%wide.region_0.1_spmd.sunk | while | flops 53078404 | bytes 184562576 | solution.py:91
  85.2 5.8 %broadcast_multiply_fusion.3 = (f32[18,10,50,128]{3,2,1,0:T(8,128)S(1)}, f32[18,10,50,128]{3,2,1,0:T(8,128)S(1)}) fusion(f32[18,10,50]{2,1,0:T(8,128)S(1)} %get-tuple-element.157, bf16[18,10,50,512]{3,2,1,0:T(8,128)(2,1)} %get-tuple-element.195, s32[]{:T(128)S(6)} %select_n.5, f32[18,10,50]{2,1,0:T(8,128)S(1)} %get-tuple-element.158), kind=kLoop, calls=%fused_computation.52.clone.1 | loop fusion | flops 3456000 | bytes 11592004 | tf_op jit(solution)/shard_map/while/body/eval_jaxpr/mul | solution.py:59
  101.7 5.2 %fusion.60 = f32[16,8,50,128]{3,2,1,0:T(8,128)S(1)} fusion(f32[16,10,50,128]{3,2,1,0:T(8,128)} %get-tuple-element.162), kind=kLoop, calls=%fused_computation.22.clone.1 | loop fusion | flops 2457600 | bytes 13107200 | tf_op jit(solution)/shard_map/while/body/eval_jaxpr/add | solution.py:47
  107.1 3.6 %fusion.63 = bf16[16,8,48,128]{3,2,1,0:T(8,128)(2,1)S(1)} fusion(f32[18,10,50,128]{3,2,1,0:T(8,128)S(1)} %get-tuple-element.161, f32[16,8,50,128]{3,2,1,0:T(8,128)S(1)} %fusion.59, f32[16,8,50,128]{3,2,1,0:T(8,128)S(1)} %fusion.60, f32[18,10,50,128]{3,2,1,0:T(8,128)S(1)} %dynamic-slice_convert_fusion.2, f32[16,8,48]{2,1,0:T(8,128)S(1)} %get-tuple-element.163, ...), kind=kLoop, calls=%fused_computation.40.clone.1 | loop fusion | flops 14155776 | bytes 26787840 | tf_op jit(solution)/shard_map/while/body/eval_jaxpr/convert_element_type | solution.py:76
  113.8 5.8 %broadcast_multiply_fusion.3 = (f32[18,10,50,128]{3,2,1,0:T(8,128)S(1)}, f32[18,10,50,128]{3,2,1,0:T(8,128)S(1)}) fusion(f32[18,10,50]{2,1,0:T(8,128)S(1)} %get-tuple-element.157, bf16[18,10,50,512]{3,2,1,0:T(8,128)(2,1)} %get-tuple-element.195, s32[]{:T(128)S(6)} %select_n.5, f32[18,10,50]{2,1,0:T(8,128)S(1)} %get-tuple-element.158), kind=kLoop, calls=%fused_computation.52.clone.1 | loop fusion | flops 3456000 | bytes 11592004 | tf_op jit(solution)/shard_map/while/body/eval_jaxpr/mul | solution.py:59
  130.3 5.2 %fusion.60 = f32[16,8,50,128]{3,2,1,0:T(8,128)S(1)} fusion(f32[16,10,50,128]{3,2,1,0:T(8,128)} %get-tuple-element.162), kind=kLoop, calls=%fused_computation.22.clone.1 | loop fusion | flops 2457600 | bytes 13107200 | tf_op jit(solution)/shard_map/while/body/eval_jaxpr/add | solution.py:47
  142.5 5.8 %broadcast_multiply_fusion.3 = (f32[18,10,50,128]{3,2,1,0:T(8,128)S(1)}, f32[18,10,50,128]{3,2,1,0:T(8,128)S(1)}) fusion(f32[18,10,50]{2,1,0:T(8,128)S(1)} %get-tuple-element.157, bf16[18,10,50,512]{3,2,1,0:T(8,128)(2,1)} %get-tuple-element.195, s32[]{:T(128)S(6)} %select_n.5, f32[18,10,50]{2,1,0:T(8,128)S(1)} %get-tuple-element.158), kind=kLoop, calls=%fused_computation.52.clone.1 | loop fusion | flops 3456000 | bytes 11592004 | tf_op jit(solution)/shard_map/while/body/eval_jaxpr/mul | solution.py:59
  158.9 5.2 %fusion.60 = f32[16,8,50,128]{3,2,1,0:T(8,128)S(1)} fusion(f32[16,10,50,128]{3,2,1,0:T(8,128)} %get-tuple-element.162), kind=kLoop, calls=%fused_computation.22.clone.1 | loop fusion | flops 2457600 | bytes 13107200 | tf_op jit(solution)/shard_map/while/body/eval_jaxpr/add | solution.py:47
  171.1 5.8 %broadcast_multiply_fusion.3 = (f32[18,10,50,128]{3,2,1,0:T(8,128)S(1)}, f32[18,10,50,128]{3,2,1,0:T(8,128)S(1)}) fusion(f32[18,10,50]{2,1,0:T(8,128)S(1)} %get-tuple-element.157, bf16[18,10,50,512]{3,2,1,0:T(8,128)(2,1)} %get-tuple-element.195, s32[]{:T(128)S(6)} %select_n.5, f32[18,10,50]{2,1,0:T(8,128)S(1)} %get-tuple-element.158), kind=kLoop, calls=%fused_computation.52.clone.1 | loop fusion | flops 3456000 | bytes 11592004 | tf_op jit(solution)/shard_map/while/body/eval_jaxpr/mul | solution.py:59
  187.5 5.2 %fusion.60 = f32[16,8,50,128]{3,2,1,0:T(8,128)S(1)} fusion(f32[16,10,50,128]{3,2,1,0:T(8,128)} %get-tuple-element.162), kind=kLoop, calls=%fused_computation.22.clone.1 | loop fusion | flops 2457600 | bytes 13107200 | tf_op jit(solution)/shard_map/while/body/eval_jaxpr/add | solution.py:47
  198.4 7.5 %convolution_bitcast_fusion = f32[512,4,128]{0,2,1:T(8,128)S(1)} fusion(bf16[4,6144,128]{2,1,0:T(8,128)(2,1)} %get-tuple-element.65, bf16[6144,512,1]{1,0,2:T(8,128)(2,1)} %bitcast.39), kind=kOutput, calls=%fused_computation.74 | convolution fusion | flops 3221225472 | bytes 13631488 | tf_op jit(solution)/shard_map/cp,bcq->pbq/dot_general | solution.py:101
  206.3 7.7 %convolution_bitcast_fusion.1 = f32[512,4,128]{0,2,1:T(8,128)S(1)} fusion(bf16[4,6144,128]{2,1,0:T(8,128)(2,1)} %get-tuple-element.64, bf16[6144,512,1]{1,0,2:T(8,128)(2,1)} %bitcast.40), kind=kOutput, calls=%fused_computation.75 | convolution fusion | flops 3221225472 | bytes 13631488 | tf_op jit(solution)/shard_map/cp,bcq->pbq/dot_general | solution.py:98
  214.7 29.5 %all_to_all.15 = f32[4,128,1024]{1,2,0:T(8,128)S(1)} all-to-all(f32[4,128,1024]{1,2,0:T(8,128)S(1)} %pad_maximum_fusion.1), channel_id=1, replica_groups=mesh['gx'=4,'gy'=16,'gz'=2] {'gx'}, dimensions={0} | all-to-all | bytes 4194304 | tf_op jit(solution)/shard_map/all_to_all | solution.py:37
  244.6 20.9 %all_to_all.16 = f32[16,8,1024]{2,1,0:T(8,128)S(1)} all-to-all(f32[16,8,1024]{2,1,0:T(8,128)S(1)} %bitcast.43), channel_id=1, replica_groups=mesh['gx'=4,'gy'=16,'gz'=2] {'gy'}, dimensions={0} | all-to-all | bytes 1048576 | tf_op jit(solution)/shard_map/all_to_all | solution.py:37
  265.5 11.1 %all_to_all.17 = f32[2,4,1024]{2,1,0:T(4,128)S(1)} all-to-all(f32[2,4,1024]{2,1,0:T(4,128)S(1)} %reshape.46), channel_id=1, replica_groups=mesh['gx'=4,'gy'=16,'gz'=2] {'gz'}, dimensions={0} | all-to-all | bytes 65536 | tf_op jit(solution)/shard_map/all_to_all | solution.py:37
  (127 shorter events, 94.4 us)
Async XLA Ops:
  1.8 9.3 %collective-permute-start.6 = (bf16[1,8,48,512]{3,2,1,0:T(8,128)(2,1)S(1)}, bf16[1,8,48,512]{3,2,1,0:T(8,128)(2,1)S(1)}, u32[]{:S(2)}, u32[]{:S(2)}) collective-permute-start(bf16[1,8,48,512]{3,2,1,0:T(8,128)(2,1)S(1)} %get-tuple-element.95), channel_id=1, source_target_pairs={{0,32},{32,64},{64,96},{1,33},{33,65},{65,97},{2,34},{34,66},{66,9... | collective-permute-start | bytes 1179656 | tf_op jit(solution)/shard_map/ppermute | solution.py:20
  3.8 7.2 %collective-permute-start = (f32[2,1,8,48]{3,2,1,0:T(8,128)S(1)}, f32[2,1,8,48]{3,2,1,0:T(8,128)S(1)}, u32[]{:S(2)}, u32[]{:S(2)}) collective-permute-start(f32[2,1,8,48]{3,2,1,0:T(8,128)S(1)} %get-tuple-element.101), channel_id=1, source_target_pairs={{0,32},{32,64},{64,96},{1,33},{33,65},{65,97},{2,34},{34,66},{66,9... | collective-permute-start | bytes 9224 | tf_op jit(solution)/shard_map/ppermute | solution.py:20
  8.5 17.7 %collective-permute-start.1 = (f32[2,1,8,48]{3,2,1,0:T(8,128)S(1)}, f32[2,1,8,48]{3,2,1,0:T(8,128)S(1)}, u32[]{:S(2)}, u32[]{:S(2)}) collective-permute-start(f32[2,1,8,48]{3,2,1,0:T(8,128)S(1)} %get-tuple-element.100), channel_id=1, source_target_pairs={{32,0},{64,32},{96,64},{33,1},{65,33},{97,65},{34,2},{66,34},{98,6... | collective-permute-start | bytes 9224 | tf_op jit(solution)/shard_map/ppermute | solution.py:22
  9.8 5.2 %collective-permute-start.7 = (bf16[1,8,48,512]{3,2,1,0:T(8,128)(2,1)S(1)}, bf16[1,8,48,512]{3,2,1,0:T(8,128)(2,1)S(1)}, u32[]{:S(2)}, u32[]{:S(2)}) collective-permute-start(bf16[1,8,48,512]{3,2,1,0:T(8,128)(2,1)S(1)} %get-tuple-element.94), channel_id=1, source_target_pairs={{32,0},{64,32},{96,64},{33,1},{65,33},{97,65},{34,2},{66,34},{98,6... | collective-permute-start | bytes 1179656 | tf_op jit(solution)/shard_map/ppermute | solution.py:22
  11.2 15.0 %copy-start.3 = (f32[2,16,8,48]{3,2,1,0:T(8,128)S(1)}, f32[2,16,8,48]{3,2,1,0:T(8,128)}, u32[]{:S(2)}) copy-start(f32[2,16,8,48]{3,2,1,0:T(8,128)} %param.5) | copy-start | bytes 147460
  15.1 2.9 %copy-start.1 = (bf16[18,8,48,512]{3,2,1,0:T(8,128)(2,1)}, bf16[18,8,48,512]{3,2,1,0:T(8,128)(2,1)S(1)}, u32[]{:S(2)}) copy-start(bf16[18,8,48,512]{3,2,1,0:T(8,128)(2,1)S(1)} %constant_dynamic-update-slice_fusion.5) | copy-start | bytes 21233668
  19.4 37.6 %collective-permute-start.9 = (bf16[18,1,48,512]{3,2,1,0:T(8,128)(2,1)}, bf16[18,1,48,512]{3,2,1,0:T(8,128)(2,1)}, u32[]{:S(2)}, u32[]{:S(2)}) collective-permute-start(bf16[18,1,48,512]{3,2,1,0:T(8,128)(2,1)} %get-tuple-element.93), channel_id=1, source_target_pairs={{2,0},{4,2},{6,4},{8,6},{10,8},{12,10},{14,12},{16,14},{18,16},{20... | collective-permute-start | bytes 2654216 | tf_op jit(solution)/shard_map/ppermute | solution.py:22
  20.7 36.3 %collective-permute-start.8 = (bf16[18,1,48,512]{3,2,1,0:T(8,128)(2,1)}, bf16[18,1,48,512]{3,2,1,0:T(8,128)(2,1)}, u32[]{:S(2)}, u32[]{:S(2)}) collective-permute-start(bf16[18,1,48,512]{3,2,1,0:T(8,128)(2,1)} %get-tuple-element.92), channel_id=1, source_target_pairs={{0,2},{2,4},{4,6},{6,8},{8,10},{10,12},{12,14},{14,16},{16,18},{18... | collective-permute-start | bytes 2654216 | tf_op jit(solution)/shard_map/ppermute | solution.py:20
  26.1 48.3 %slice-start = ((s8[7077888]{0:T(1024)(128)(4,1)}), s8[2883584]{0:T(1024)(128)(4,1)S(1)}, s32[]{:S(2)}) async-start(s8[7077888]{0:T(1024)(128)(4,1)} %bitcast.41), calls=%async_computation.3 | async-start | bytes 5767168
  26.2 14.2 %collective-permute-start.3 = (f32[2,18,1,48]{3,2,1,0:T(1,128)S(1)}, f32[2,18,1,48]{3,2,1,0:T(1,128)S(1)}, u32[]{:S(2)}, u32[]{:S(2)}) collective-permute-start(f32[2,18,1,48]{3,2,1,0:T(1,128)S(1)} %get-tuple-element.99), channel_id=1, source_target_pairs={{2,0},{4,2},{6,4},{8,6},{10,8},{12,10},{14,12},{16,14},{18,16},{20... | collective-permute-start | bytes 20744 | tf_op jit(solution)/shard_map/ppermute | solution.py:22
  27.8 14.4 %collective-permute-start.2 = (f32[2,18,1,48]{3,2,1,0:T(1,128)S(1)}, f32[2,18,1,48]{3,2,1,0:T(1,128)S(1)}, u32[]{:S(2)}, u32[]{:S(2)}) collective-permute-start(f32[2,18,1,48]{3,2,1,0:T(1,128)S(1)} %get-tuple-element.98), channel_id=1, source_target_pairs={{0,2},{2,4},{4,6},{6,8},{8,10},{10,12},{12,14},{14,16},{16,18},{18... | collective-permute-start | bytes 20744 | tf_op jit(solution)/shard_map/ppermute | solution.py:20
  43.2 10.6 %collective-permute-start.5 = (f32[2,18,10,1]{3,2,1,0:T(8,128)}, f32[2,18,10,1]{3,2,1,0:T(8,128)S(1)}, u32[]{:S(2)}, u32[]{:S(2)}) collective-permute-start(f32[2,18,10,1]{3,2,1,0:T(8,128)} %get-tuple-element.97), channel_id=1, source_target_pairs={{1,0},{3,2},{5,4},{7,6},{9,8},{11,10},{13,12},{15,14},{17,16},{19,... | collective-permute-start | bytes 4328 | tf_op jit(solution)/shard_map/ppermute | solution.py:22
  44.5 11.2 %collective-permute-start.4 = (f32[2,18,10,1]{3,2,1,0:T(8,128)}, f32[2,18,10,1]{3,2,1,0:T(8,128)}, u32[]{:S(2)}, u32[]{:S(2)}) collective-permute-start(f32[2,18,10,1]{3,2,1,0:T(8,128)} %get-tuple-element.96), channel_id=1, source_target_pairs={{0,1},{2,3},{4,5},{6,7},{8,9},{10,11},{12,13},{14,15},{16,17},{18,... | collective-permute-start | bytes 4328 | tf_op jit(solution)/shard_map/ppermute | solution.py:20
  53.8 0.7 copy-start.2
  57.0 17.5 %slice-start.1 = ((s8[7077888]{0:T(1024)(128)(4,1)}), s8[4194304]{0:T(1024)(128)(4,1)S(1)}, s32[]{:S(2)}) async-start(s8[7077888]{0:T(1024)(128)(4,1)} %bitcast.41), calls=%async_computation.4 | async-start | bytes 8388608
  59.6 13.1 %collective-permute-start.11 = (bf16[18,10,1,512]{3,2,1,0:T(2,128)(2,1)S(1)}, bf16[18,10,1,512]{3,2,1,0:T(2,128)(2,1)S(1)}, u32[]{:S(2)}, u32[]{:S(2)}) collective-permute-start(bf16[18,10,1,512]{3,2,1,0:T(2,128)(2,1)S(1)} %get-tuple-element.91), channel_id=1, source_target_pairs={{1,0},{3,2},{5,4},{7,6},{9,8},{11,10},{13,12},{15,14},{17,16},{19,... | collective-permute-start | bytes 552968 | tf_op jit(solution)/shard_map/ppermute | solution.py:22
  60.9 13.6 %collective-permute-start.10 = (bf16[18,10,1,512]{3,2,1,0:T(2,128)(2,1)S(1)}, bf16[18,10,1,512]{3,2,1,0:T(2,128)(2,1)S(1)}, u32[]{:S(2)}, u32[]{:S(2)}) collective-permute-start(bf16[18,10,1,512]{3,2,1,0:T(2,128)(2,1)S(1)} %get-tuple-element.90), channel_id=1, source_target_pairs={{0,1},{2,3},{4,5},{6,7},{8,9},{10,11},{12,13},{14,15},{16,17},{18,... | collective-permute-start | bytes 552968 | tf_op jit(solution)/shard_map/ppermute | solution.py:20
  107.0 3.6 %copy-start = (bf16[16,8,48,128]{3,2,1,0:T(8,128)(2,1)S(1)}, bf16[16,8,48,128]{3,2,1,0:T(8,128)(2,1)}, u32[]{:S(2)}) copy-start(bf16[16,8,48,128]{3,2,1,0:T(8,128)(2,1)} %fusion.57) | copy-start | bytes 4718596 | tf_op jit(solution)/shard_map/while
  135.7 3.6 %copy-start = (bf16[16,8,48,128]{3,2,1,0:T(8,128)(2,1)S(1)}, bf16[16,8,48,128]{3,2,1,0:T(8,128)(2,1)}, u32[]{:S(2)}) copy-start(bf16[16,8,48,128]{3,2,1,0:T(8,128)(2,1)} %fusion.57) | copy-start | bytes 4718596 | tf_op jit(solution)/shard_map/while
  164.3 3.6 %copy-start = (bf16[16,8,48,128]{3,2,1,0:T(8,128)(2,1)S(1)}, bf16[16,8,48,128]{3,2,1,0:T(8,128)(2,1)}, u32[]{:S(2)}) copy-start(bf16[16,8,48,128]{3,2,1,0:T(8,128)(2,1)} %fusion.57) | copy-start | bytes 4718596 | tf_op jit(solution)/shard_map/while
  192.9 3.6 %copy-start = (bf16[16,8,48,128]{3,2,1,0:T(8,128)(2,1)S(1)}, bf16[16,8,48,128]{3,2,1,0:T(8,128)(2,1)}, u32[]{:S(2)}) copy-start(bf16[16,8,48,128]{3,2,1,0:T(8,128)(2,1)} %fusion.57) | copy-start | bytes 4718596 | tf_op jit(solution)/shard_map/while
where the time goes:
time: 279 us; the launch traced here: 277 us
  other arithmetic  116 us (42%)
  blocking collectives  61.6 us (22%)
  starting transfers between devices  37 us (13%)
  local copies, waits for them, and re-layouts  23 us (8%)
  waiting for transfers between devices  20.8 us (7%)
  matrix products  15.2 us (5%)
  loops' own time  3.05 us (1%)
    all_to_all x3, blocking collectives, sum_at_owner(): parts = lax.all_to_all(split_up(x, dim, devices), axis, 0, 0, tiled=True)  61.6 us
    add x37, other arithmetic, three_taps(): field = side * (lower + upper) + middle * centre  42.4 us
    ppermute x6, starting transfers between devices, with_halo(): lax.ppermute(tail, axis, [(i, (i + 1) % count) for i in range(ends)])  29 us
    convert_element_type x8, other arithmetic, apply_operators(): return (stiff_sum.astype(jnp.bfloat16), mass_sum.astype(jnp.bfloat16))  26.6 us
    mul x4, other arithmetic, apply_operators(): rho_values = rho[..., None] * values  23.2 us
    ppermute x6, waiting for transfers between devices, with_halo(): lax.ppermute(head, axis, [((i + 1) % count, i) for i in range(ends)])  16.2 us
    concatenate x3, other arithmetic, with_halo(): jnp.concatenate([lax.ppermute(tail, axis, [(i, (i + 1) % count) for i in...  10.9 us
    convert_element_type x4, other arithmetic, apply_operators(): values = padded.astype(jnp.float32)  8.28 us
  transfers between devices with their start and end apart: 12, of which 6 were waited for; matrix products, arithmetic and copies ran while one was open for 3% of the time, Pallas kernels for 0%

commit v1 on v0

v1 whole, which is shorter than its diff:
```python
import functools

import jax
import jax.numpy as jnp
import numpy as np
from jax import lax
from jax.experimental import pallas as pl
from jax.experimental.pallas import tpu as pltpu
from jax.sharding import PartitionSpec as P

MESH = pl.DeviceIdType.MESH
F32 = jnp.float32
BF16 = jnp.bfloat16
HIGH = lax.Precision.HIGHEST

SX, SY, SZ, K = 16, 8, 48, 512
PX, PY = SX + 2, SY + 2
HALF = PY // 2
CELLS = 64 * 128 * 96
DIM0 = (((0,), (0,)), ((), ()))


def constants():
    rows = HALF * SZ
    tz = np.zeros((rows, rows), np.float32)
    for r in range(rows):
        for c in (r - 1, r, r + 1):
            if 0 <= c < rows and c // SZ == r // SZ:
                tz[r, c] = 2.0 if c == r else 1.0
    sel = np.zeros((SX * SY, 256), np.float32)
    txy = np.zeros((SX * SY, 256), np.float32)
    for x in range(SX):
        for y in range(SY):
            row = x * SY + y
            sel[row, (x + 1) * PY + y + 1] = 1.0
            for dx in (-1, 0, 1):
                for dy in (-1, 0, 1):
                    txy[row, (x + 1 + dx) * PY + y + 1 + dy] = (2 - abs(dx)) * (2 - abs(dy))
    places = {}
    for x in range(SX):
        for y in range(SY):
            places[(x, y)] = x * SY + y
    for x in range(SX):
        places[(x, SY)] = 128 + x
        places[(x, -1)] = 144 + x
    for y in range(SY):
        places[(SX, y)] = 160 + y
        places[(-1, y)] = 176 + y
    places[(SX, SY)] = 192
    places[(SX, -1)] = 208 + 7
    places[(-1, SY)] = 224
    places[(-1, -1)] = 240 + 7
    t2 = np.zeros((128, 256), np.float32)
    t4 = np.zeros((128, 256), np.float32)
    for x in range(SX):
        for y in range(SY):
            for dx in (-1, 0, 1):
                for dy in (-1, 0, 1):
                    place = places[(x + dx, y + dy)]
                    t2[x * SY + y, place] = (2 - abs(dx)) * (2 - abs(dy))
                    t4[x * SY + y, place] = (4 - 3 * abs(dx)) * (4 - 3 * abs(dy))
    pick = np.zeros((64, 128), np.float32)
    for x in range(SX):
        pick[x, x * SY] = 1.0
        pick[16 + x, x * SY + 7] = 1.0
    for y in range(SY):
        pick[32 + y, y] = 1.0
        pick[48 + y, 15 * SY + y] = 1.0
    return tz, sel, txy, t2, t4, np.ascontiguousarray(t2.T), pick


def local_kernel(
    v_hbm, mat, tz_ref, sel_ref, txy_ref, t2_ref, t4_ref, t2t_ref, pick_ref, out,
    vp, az, bz, ya, yb, xbuf, vt, coef, acc, zf, zs, zh, zface,
    own_sem, up_send, dn_send, up_recv, dn_recv, side_send, side_recv, z_send, z_recv,
):
    gx, gy, gz = lax.axis_index("gx"), lax.axis_index("gy"), lax.axis_index("gz")
    other = 1 - gz

    def at(dx, dy, z):
        return {"gx": lax.rem(gx + dx + 4, 4), "gy": lax.rem(gy + dy + 16, 16), "gz": z}

    around = [(dx, dy) for dx in (-1, 0, 1) for dy in (-1, 0, 1)]
    barrier = pltpu.get_barrier_semaphore()
    for dx, dy in around:
        if (dx, dy) != (0, 0):
            pl.semaphore_signal(barrier, inc=1, device_id=at(dx, dy, gz), device_id_type=MESH)
        pl.semaphore_signal(barrier, inc=1, device_id=at(dx, dy, other), device_id_type=MESH)

    def own_copy(x):
        return pltpu.make_async_copy(v_hbm.at[x], vp.at[x + 1, pl.ds(1, SY)], own_sem.at[x])

    @pl.loop(0, SX)
    def _(x):
        own_copy(x).start()

    def has(dx, dy):
        ok = jnp.bool_(True)
        if dx == 1:
            ok = jnp.logical_and(ok, gx < 3)
        if dx == -1:
            ok = jnp.logical_and(ok, gx > 0)
        if dy == 1:
            ok = jnp.logical_and(ok, gy < 15)
        if dy == -1:
            ok = jnp.logical_and(ok, gy > 0)
        return ok

    def remote(src, dst, send, recv, where):
        return pltpu.make_async_remote_copy(
            src_ref=src, dst_ref=dst, send_sem=send, recv_sem=recv, device_id=where, device_id_type=MESH
        )

    def up(x):
        return remote(v_hbm.at[x, SY - 1], vp.at[x + 1, 0], up_send.at[x], up_recv.at[x], at(0, 1, gz))

    def down(x):
        return remote(v_hbm.at[x, 0], vp.at[x + 1, PY - 1], dn_send.at[x], dn_recv.at[x], at(0, -1, gz))

    def side(index):
        dx, dy = sides[index]
        src_x = SX - 1 if dx == 1 else 0
        dst_x = 0 if dx == 1 else PX - 1
        if dy == 0:
            src, dst = v_hbm.at[src_x], vp.at[dst_x, pl.ds(1, SY)]
        elif dy == 1:
            src, dst = v_hbm.at[src_x, SY - 1], vp.at[dst_x, 0]
        else:
            src, dst = v_hbm.at[src_x, 0], vp.at[dst_x, PY - 1]
        return remote(src, dst, side_send.at[index], side_recv.at[index], at(dx, dy, gz))

    sides = [(1, 0), (1, 1), (1, -1), (-1, 0), (-1, 1), (-1, -1)]

    @pl.when(jnp.logical_not(has(0, -1)))
    def _():
        vp[:, 0] = jnp.zeros((PX, SZ, K), BF16)

    @pl.when(jnp.logical_not(has(0, 1)))
    def _():
        vp[:, PY - 1] = jnp.zeros((PX, SZ, K), BF16)

    @pl.when(jnp.logical_not(has(-1, 0)))
    def _():
        vp[0] = jnp.zeros((PY, SZ, K), BF16)

    @pl.when(jnp.logical_not(has(1, 0)))
    def _():
        vp[PX - 1] = jnp.zeros((PY, SZ, K), BF16)

    zrows = [(0, 0, 0, 128)]
    zrows += [(0, 1, 128, 16), (0, -1, 144, 16), (1, 0, 160, 16), (-1, 0, 176, 16)]
    zrows += [(1, 1, 192, 16), (1, -1, 208, 16), (-1, 1, 224, 16), (-1, -1, 240, 16)]
    for dx, dy, first, count in zrows[1:]:

        @pl.when(jnp.logical_not(has(dx, dy)))
        def _():
            zh[pl.ds(first, count)] = jnp.zeros((count, K), BF16)

    pl.semaphore_wait(barrier, 17)

    @pl.when(has(1, 0))
    def _():
        side(0).start()

    @pl.when(has(-1, 0))
    def _():
        side(3).start()

    for index in (1, 2, 4, 5):

        @pl.when(has(*sides[index]))
        def _():
            side(index).start()

    @pl.loop(0, SX)
    def _(x):
        @pl.when(has(0, 1))
        def _():
            up(x).start()

        @pl.when(has(0, -1))
        def _():
            down(x).start()

    kappa = mat[0].reshape(SX * SY, SZ)
    rho = mat[1].reshape(SX * SY, SZ)
    own_kappa = lax.dot_general(kappa, sel_ref[...], DIM0, precision=HIGH, preferred_element_type=F32)
    own_rho = lax.dot_general(rho, sel_ref[...], DIM0, precision=HIGH, preferred_element_type=F32)
    near = lax.dot_general(kappa, txy_ref[...], DIM0, precision=HIGH, preferred_element_type=F32)
    edge_row = jnp.zeros((1, 256), F32)
    near = (
        jnp.concatenate([edge_row, near[:-1]], axis=0)
        + 2.0 * near
        + jnp.concatenate([near[1:], edge_row], axis=0)
    )
    alpha = 2.0 * own_kappa + near * (1.0 / 32.0)
    beta = own_kappa * (1.0 / 16.0)
    for xp in range(PX):
        span = slice(xp * PY, xp * PY + PY)
        coef[xp, 0, :, 0:PY] = alpha[:, span]
        coef[xp, 1, :, 0:PY] = beta[:, span]
        coef[xp, 2, :, 0:PY] = own_rho[:, span]

    @pl.loop(0, SX)
    def _(x):
        own_copy(x).wait()
        low = vp[x + 1, 1 : 1 + SY, 0:16, :].astype(F32)
        high = vp[x + 1, 1 : 1 + SY, SZ - 16 : SZ, :].astype(F32)
        spot = lax.broadcasted_iota(jnp.int32, (1, 16, 1), 1)
        low = jnp.sum(jnp.where(spot == 0, low, 0.0), axis=1)
        high = jnp.sum(jnp.where(spot == 15, high, 0.0), axis=1)
        zf[pl.ds(pl.multiple_of(x * SY, SY), SY)] = jnp.where(gz == 0, high, low)

    zface[...] = zf[...].astype(BF16)
    zs[...] = jnp.dot(pick_ref[...], zface[...], preferred_element_type=F32).astype(BF16)

    def zcopy(index, dx, dy):
        first, count = zrows[index][2:]
        if (dx, dy) == (0, 0):
            src = zface
        elif dx == 0:
            src = zs.at[pl.ds(16 if dy == 1 else 0, 16)]
        else:
            src = zs.at[pl.ds(48 if dx == 1 else 32, 16)]
        return remote(
            src, zh.at[pl.ds(first, count)], z_send.at[index], z_recv.at[index], at(dx, dy, other)
        )

    for index, (dx, dy, _, _) in enumerate(zrows):

        @pl.when(has(-dx, -dy))
        def _():
            zcopy(index, -dx, -dy).start()

    acc[...] = jnp.zeros_like(acc)

    def wait_plane(xp):
        @pl.when(jnp.logical_and(xp >= 1, xp <= SX))
        def _():
            @pl.when(has(0, -1))
            def _():
                up(xp - 1).wait_recv()

            @pl.when(has(0, 1))
            def _():
                down(xp - 1).wait_recv()

        @pl.when(xp == 0)
        def _():
            for index in (0, 1, 2):
                dx, dy = sides[index]

                @pl.when(has(-dx, -dy))
                def _():
                    side(index).wait_recv()

        @pl.when(xp == PX - 1)
        def _():
            for index in (3, 4, 5):
                dx, dy = sides[index]

                @pl.when(has(-dx, -dy))
                def _():
                    side(index).wait_recv()

    def plane_stage(xp, slot):
        wait_plane(xp)
        for b in range(2):
            for c in range(2):
                lanes = slice(256 * c, 256 * c + 256)
                own = vp[xp, HALF * b : HALF * b + HALF, :, lanes]
                a = jnp.dot(
                    tz_ref[...], own.reshape(HALF * SZ, 256), preferred_element_type=F32
                ).astype(BF16).reshape(HALF, SZ, 256)
                az[HALF * b : HALF * b + HALF, :, lanes] = a
                bz[HALF * b : HALF * b + HALF, :, lanes] = a + (own + own)
        for y in range(SY):
            mid = az[y + 1]
            ya[slot, y] = (az[y] + az[y + 2]) + (mid + mid)
            mid = bz[y + 1]
            yb[slot, y] = (bz[y] + bz[y + 2]) + BF16(4.0) * mid

    def cell_stage(x):
        s0, s1, s2 = lax.rem(x, 3), lax.rem(x + 1, 3), lax.rem(x + 2, 3)
        for y in range(SY):
            al = coef[x + 1, 0, :, y + 1 : y + 2]
            be = coef[x + 1, 1, :, y + 1 : y + 2]
            ro = coef[x + 1, 2, :, y + 1 : y + 2]
            mid = ya[s1, y]
            u = (ya[s0, y] + ya[s2, y]) + (mid + mid)
            mid = yb[s1, y]
            m = (yb[s0, y] + yb[s2, y]) + BF16(4.0) * mid
            own = vp[x + 1, y + 1].astype(F32)
            xbuf[pl.ds(y * SZ, SZ), 0:K] = (al * own - be * u.astype(F32)).astype(BF16)
            xbuf[pl.ds(y * SZ, SZ), K : 2 * K] = (ro * m.astype(F32)).astype(BF16)
        vt[...] = vp[x + 1, 1 : 1 + SY].reshape(SY * SZ, K).T
        for c in range(4):
            lanes = slice(256 * c, 256 * c + 256)
            acc[:, lanes] += jnp.dot(vt[...], xbuf[:, lanes], preferred_element_type=F32)

    plane_stage(jnp.int32(0), jnp.int32(0))
    plane_stage(jnp.int32(1), jnp.int32(1))

    @pl.loop(0, SX)
    def _(x):
        plane_stage(x + 2, lax.rem(x + 2, 3))
        cell_stage(x)

    def halo_rows(xp, yp):
        return coef[xp, 0, :, yp : yp + 1] * vp[xp, yp].astype(F32)

    for xp in (0, PX - 1):
        for y in range(SY):
            xbuf[y * SZ : y * SZ + SZ, 0:K] = halo_rows(xp, y + 1).astype(BF16)
        vt[...] = vp[xp, 1 : 1 + SY].reshape(SY * SZ, K).T
        for c in range(2):
            lanes = slice(256 * c, 256 * c + 256)
            acc[:, lanes] += jnp.dot(vt[...], xbuf[:, lanes], preferred_element_type=F32)
    for yp in (0, PY - 1):
        @pl.loop(0, 3)
        def _(part):
            for i in range(6):
                xbuf[i * SZ : i * SZ + SZ, 0:K] = halo_rows(part * 6 + i, yp).astype(BF16)
            turned = vp[pl.ds(part * 6, 6), yp].reshape(6 * SZ, K).T
            for c in range(2):
                lanes = slice(256 * c, 256 * c + 256)
                acc[:, lanes] += jnp.dot(turned, xbuf[0 : 6 * SZ, lanes], preferred_element_type=F32)

    for index, (dx, dy, _, _) in enumerate(zrows):

        @pl.when(has(dx, dy))
        def _():
            zcopy(index, -dx, -dy).wait_recv()

    lane = lax.broadcasted_iota(jnp.int32, (SX * SY, SZ), 1)
    at_edge = lane == jnp.where(gz == 0, SZ - 1, 0)
    kappa_edge = jnp.sum(jnp.where(at_edge, kappa, 0.0), axis=1, keepdims=True)
    rho_edge = jnp.sum(jnp.where(at_edge, rho, 0.0), axis=1, keepdims=True)
    far = zh[...]
    du = jnp.dot(t2_ref[...], far, preferred_element_type=F32)
    dm = jnp.dot(t4_ref[...], far, preferred_element_type=F32)
    xbuf[0:128, 0:K] = (kappa_edge * (-1.0 / 16.0) * du).astype(BF16)
    xbuf[0:128, K : 2 * K] = (rho_edge * dm).astype(BF16)
    turned = zface[...].T
    for c in range(4):
        lanes = slice(256 * c, 256 * c + 256)
        acc[:, lanes] += jnp.dot(turned, xbuf[0:128, lanes], preferred_element_type=F32)
    reach = jnp.dot(
        t2t_ref[...], jnp.broadcast_to(kappa_edge, (128, 128)), precision=HIGH, preferred_element_type=F32
    ) * (1.0 / 32.0)
    for c in range(4):
        lanes = slice(128 * c, 128 * c + 128)
        xbuf[0:256, lanes] = (reach * far[:, lanes].astype(F32)).astype(BF16)
    turned = far.T
    for c in range(2):
        lanes = slice(256 * c, 256 * c + 256)
        acc[:, lanes] += jnp.dot(turned, xbuf[0:256, lanes], preferred_element_type=F32)

    for half, scale in ((0, 0.5 / CELLS), (1, 0.5 / (216.0 * CELLS))):
        for i in range(4):
            for j in range(i, 4):
                rows = slice(128 * i, 128 * i + 128)
                cols = slice(128 * j, 128 * j + 128)
                there = slice(K * half + 128 * j, K * half + 128 * j + 128)
                back = slice(K * half + 128 * i, K * half + 128 * i + 128)
                both = (acc[rows, there] + acc[cols, back].T) * scale
                out[rows, there] = both
                if i != j:
                    out[cols, back] = both.T

    @pl.loop(0, SX)
    def _(x):
        @pl.when(has(0, 1))
        def _():
            up(x).wait_send()

        @pl.when(has(0, -1))
        def _():
            down(x).wait_send()

    for index in range(6):

        @pl.when(has(*sides[index]))
        def _():
            side(index).wait_send()

    for index, (dx, dy, _, _) in enumerate(zrows):

        @pl.when(has(-dx, -dy))
        def _():
            zcopy(index, -dx, -dy).wait_send()


def local_products(eigvecs, material):
    tz, sel, txy, t2, t4, t2t, pick = constants()
    small = (
        jnp.asarray(tz, BF16), jnp.asarray(sel), jnp.asarray(txy), jnp.asarray(t2, BF16),
        jnp.asarray(t4, BF16), jnp.asarray(t2t), jnp.asarray(pick, BF16),
    )
    vmem = pl.BlockSpec(memory_space=pltpu.VMEM)
    dma = pltpu.SemaphoreType.DMA
    return pl.pallas_call(
        local_kernel,
        out_shape=jax.ShapeDtypeStruct((K, 2 * K), F32),
        in_specs=[pl.BlockSpec(memory_space=pl.ANY)] + [vmem] * 8,
        out_specs=vmem,
        scratch_shapes=[
            pltpu.VMEM((PX, PY, SZ, K), BF16),
            pltpu.VMEM((PY, SZ, K), BF16),
            pltpu.VMEM((PY, SZ, K), BF16),
            pltpu.VMEM((3, SY, SZ, K), BF16),
            pltpu.VMEM((3, SY, SZ, K), BF16),
            pltpu.VMEM((SY * SZ, 2 * K), BF16),
            pltpu.VMEM((K, SY * SZ), BF16),
            pltpu.VMEM((PX, 3, SZ, 128), F32),
            pltpu.VMEM((K, 2 * K), F32),
            pltpu.VMEM((SX * SY, K), F32),
            pltpu.VMEM((64, K), BF16),
            pltpu.VMEM((256, K), BF16),
            pltpu.VMEM((SX * SY, K), BF16),
            dma((SX,)), dma((SX,)), dma((SX,)), dma((SX,)), dma((SX,)),
            dma((6,)), dma((6,)), dma((9,)), dma((9,)),
        ],
        compiler_params=pltpu.CompilerParams(
            collective_id=0, has_side_effects=True, vmem_limit_bytes=60 * 1024 * 1024
        ),
    )(eigvecs, material, *small)


def split_up(x, dim, devices):
    dims = x.shape
    parts = x.reshape(*dims[:dim], devices, dims[dim] // devices, *dims[dim + 1 :])
    return jnp.moveaxis(parts, dim, 0)


def sum_at_owner(x, axis, dim):
    devices = lax.axis_size(axis)
    parts = lax.all_to_all(split_up(x, dim, devices), axis, 0, 0, tiled=True)
    return jnp.sum(parts, axis=0)


def per_device(eigvecs, material):
    both = local_products(eigvecs, material)
    summed = sum_at_owner(sum_at_owner(sum_at_owner(both, "gx", 0), "gy", 0), "gz", 0)
    return summed[:, :K], summed[:, K:]


def solution(mesh):
    return jax.shard_map(
        per_device,
        mesh=mesh,
        in_specs=(P("gx", "gy", "gz", None), P(None, "gx", "gy", "gz")),
        out_specs=(P(("gx", "gy", "gz"), None), P(("gx", "gy", "gz"), None)),
        check_vma=False,
    )
```

time: 279 us -> 102 us (0.37)
  other arithmetic: 116 us -> 0.23 us
  Pallas kernels: 0 us -> 43.3 us
  starting transfers between devices: 37 us -> 0 us
  local copies, waits for them, and re-layouts: 23 us -> 0.62 us
  waiting for transfers between devices: 20.8 us -> 0 us
  matrix products: 15.2 us -> 0 us
  blocking collectives: 61.6 us -> 56.8 us
  loops' own time: 3.05 us -> 0 us
    pallas_call x0 -> x1, Pallas kernels: none -> 43.3 us  [local_products(): pl.pallas_call(local_kernel, out_shape=jax.ShapeDtypeStruct((K, 2 * K), F...]
    add x37 -> x0, other arithmetic: 42.4 us -> none  [three_taps(): field = side * (lower + upper) + middle * centre]
    ppermute x12 -> x0, starting transfers between devices: 37 us -> none  [the longest x6 29 us: with_halo(): lax.ppermute(tail, axis, [(i, (i + 1) % count) for i in range(ends)])]
    convert_element_type x12 -> x0, other arithmetic: 34.9 us -> none  [the longest x8 26.6 us: apply_operators(): return (stiff_sum.astype(jnp.bfloat16), mass_sum.astype(jnp.bfloat16))]
    mul x12 -> x0, other arithmetic: 24 us -> none  [the longest x4 23.2 us: apply_operators(): rho_values = rho[..., None] * values]
    ppermute x12 -> x0, waiting for transfers between devices: 20.8 us -> none  [the longest x6 16.2 us: with_halo(): lax.ppermute(head, axis, [((i + 1) % count, i) for i in range(ends)])]
    dot_general x2 -> x0, matrix products: 15.2 us -> none  [the longest x1 7.74 us: per_device(): jnp.einsum('cp,bcq->pbq', flat_vectors, stiff_blocks, preferred_element_t...]
    concatenate x4 -> x0, other arithmetic: 11 us -> none  [the longest x3 10.9 us: with_halo(): jnp.concatenate([lax.ppermute(tail, axis, [(i, (i + 1) % count) for i in...]
  transfers between devices with their start and end apart: 12 -> 0, of which waited for: 6 -> 0; matrix products, arithmetic and copies ran while one was open for 3% -> 0% of each run, Pallas kernels for 0% -> 0%
where the time goes in v1:
time: 102 us
  blocking collectives  56.8 us (56%)
  Pallas kernels  43.3 us (42%)
    all_to_all x3, blocking collectives, sum_at_owner(): parts = lax.all_to_all(split_up(x, dim, devices), axis, 0, 0, tiled=True)  56.8 us
    pallas_call x1, Pallas kernels, local_products(): pl.pallas_call(local_kernel, out_shape=jax.ShapeDtypeStruct((K, 2 * K), F...  43.3 us

profile of v1, /device:TPU:0, one launch (start us, length us, event | category | flops | bytes accessed | tf_op | source)
XLA Modules:
  0.0 101.6 jit_solution(18292302415614991336)
XLA Ops:
  0.6 43.3 %shard_map.104 = f32[512,1024]{1,0:T(8,128)} custom-call(bf16[16,8,48,512]{3,2,1,0:T(8,128)(2,1)} %v_hbm.1, f32[2,16,8,48]{3,2,1,0:T(8,128)} %mat.1, bf16[240,240]{1,0:T(8,128)(2,1)} %constant.16.clone.tz_ref, f32[128,256]{1,0:T(8,128)} %constant.17.clone.sel_ref, f32[128,256]{1,0:T(8,128)} %constant.18.clone.txy_ref, ...), custom_call_target="tpu_custom_call" | custom-call | tf_op jit(solution)/shard_map/pallas_call | solution.py:402
  44.0 33.7 %all_to_all.15 = f32[4,128,1024]{2,1,0:T(8,128)S(1)} all-to-all(f32[4,128,1024]{2,1,0:T(8,128)} %bitcast.2), channel_id=1, replica_groups=mesh['gx'=4,'gy'=16,'gz'=2] {'gx'}, dimensions={0} | all-to-all | bytes 4194304 | tf_op jit(solution)/shard_map/all_to_all | solution.py:438
  77.7 0.2 reduce_sum.27
  77.9 15.1 %all_to_all.16 = f32[16,8,1024]{2,1,0:T(8,128)S(1)} all-to-all(f32[16,8,1024]{2,1,0:T(8,128)S(1)} %bitcast.3), channel_id=1, replica_groups=mesh['gx'=4,'gy'=16,'gz'=2] {'gy'}, dimensions={0} | all-to-all | bytes 1048576 | tf_op jit(solution)/shard_map/all_to_all | solution.py:438
  93.0 8.0 %all_to_all.17 = f32[2,4,1024]{2,1,0:T(4,128)S(1)} all-to-all(f32[2,4,1024]{2,1,0:T(4,128)S(1)} %reshape.15), channel_id=1, replica_groups=mesh['gx'=4,'gy'=16,'gz'=2] {'gz'}, dimensions={0} | all-to-all | bytes 65536 | tf_op jit(solution)/shard_map/all_to_all | solution.py:438
  101.0 0.6 fusion
  (3 shorter events, 0.1 us)

commit v2 on v1

--- a/solution.py
+++ b/solution.py
@@ -18,6 +18,8 @@
 HALF = PY // 2
 CELLS = 64 * 128 * 96
 DIM0 = (((0,), (0,)), ((), ()))
+COLORS = ((0, 384), (384, 384), (768, 256))
+ORDERS = ("xyz", "yzx", "zxy")
 
 
 def constants():
@@ -70,10 +72,13 @@
 
 
 def local_kernel(
-    v_hbm, mat, tz_ref, sel_ref, txy_ref, t2_ref, t4_ref, t2t_ref, pick_ref, out,
+    v_hbm, mat, tz_ref, sel_ref, txy_ref, t2_ref, t4_ref, t2t_ref, pick_ref, stiff_out, mass_out,
     vp, az, bz, ya, yb, xbuf, vt, coef, acc, zf, zs, zh, zface,
     own_sem, up_send, dn_send, up_recv, dn_recv, side_send, side_recv, z_send, z_recv,
+    sym, core_in, *ring,
 ):
+    core_send, core_recv, ring_send, ring_recv = ring[-4:]
+    ring = ring[:-4]
     gx, gy, gz = lax.axis_index("gx"), lax.axis_index("gy"), lax.axis_index("gz")
     other = 1 - gz
 
@@ -86,6 +91,28 @@
         if (dx, dy) != (0, 0):
             pl.semaphore_signal(barrier, inc=1, device_id=at(dx, dy, gz), device_id_type=MESH)
         pl.semaphore_signal(barrier, inc=1, device_id=at(dx, dy, other), device_id_type=MESH)
+
+    core, z_lo = lax.rem(gx, 2), lax.div(gx, 2)
+    ring_x, ring_y = lax.div(gy, 4), lax.rem(gy, 4)
+    ring_z = 2 * gz + z_lo
+    partner = {"gx": gx + 1 - 2 * core, "gy": gy, "gz": gz}
+
+    def ring_place(dim, k):
+        mine = {"x": ring_x, "y": ring_y, "z": ring_z}[dim]
+        return lax.rem(mine + k, 4)
+
+    def ring_peer(dim, k):
+        spot = ring_place(dim, k)
+        if dim == "x":
+            return {"gx": gx, "gy": 4 * spot + ring_y, "gz": gz}
+        if dim == "y":
+            return {"gx": gx, "gy": 4 * ring_x + spot, "gz": gz}
+        return {"gx": 2 * lax.rem(spot, 2) + core, "gy": gy, "gz": lax.div(spot, 2)}
+
+    pl.semaphore_signal(barrier, inc=1, device_id=partner, device_id_type=MESH)
+    for dim in "xyz":
+        for k in (1, 2, 3):
+            pl.semaphore_signal(barrier, inc=1, device_id=ring_peer(dim, k), device_id_type=MESH)
 
     def own_copy(x):
         return pltpu.make_async_copy(v_hbm.at[x], vp.at[x + 1, pl.ds(1, SY)], own_sem.at[x])
@@ -156,7 +183,7 @@
         def _():
             zh[pl.ds(first, count)] = jnp.zeros((count, K), BF16)
 
-    pl.semaphore_wait(barrier, 17)
+    pl.semaphore_wait(barrier, 27)
 
     @pl.when(has(1, 0))
     def _():
@@ -356,6 +383,20 @@
         lanes = slice(256 * c, 256 * c + 256)
         acc[:, lanes] += jnp.dot(turned, xbuf[0:256, lanes], preferred_element_type=F32)
 
+    def core_copy(c):
+        first, width = COLORS[c]
+        cols = pl.ds(first, width)
+        return remote(
+            sym.at[1 - core, :, :, :, :, :, cols], core_in.at[:, :, :, :, :, cols],
+            core_send.at[c], core_recv.at[c], partner,
+        )
+
+    def put(gx_row, col, block):
+        for part in range(32):
+            sym[
+                gx_row % 2, gx_row // 2, part // 8, part // 2 % 4, part % 2, :, col : col + 128
+            ] = block[4 * part : 4 * part + 4]
+
     for half, scale in ((0, 0.5 / CELLS), (1, 0.5 / (216.0 * CELLS))):
         for i in range(4):
             for j in range(i, 4):
@@ -364,9 +405,76 @@
                 there = slice(K * half + 128 * j, K * half + 128 * j + 128)
                 back = slice(K * half + 128 * i, K * half + 128 * i + 128)
                 both = (acc[rows, there] + acc[cols, back].T) * scale
-                out[rows, there] = both
+                put(i, K * half + 128 * j, both)
                 if i != j:
-                    out[cols, back] = both.T
+                    put(j, K * half + 128 * i, both.T)
+        if half == 0:
+            core_copy(0).start()
+        else:
+            core_copy(1).start()
+            core_copy(2).start()
+
+    held = [[ring[6 * c + 2 * s] for s in range(3)] for c in range(3)]
+    landed = [[ring[6 * c + 2 * s + 1] for s in range(3)] for c in range(3)]
+
+    def piece(c, s, spot):
+        ref, dim, left = held[c][s], ORDERS[c][s], ORDERS[c][s:]
+        index = []
+        for name in ("z_lo", "x", "y", "z_hi"):
+            if name[0] not in left:
+                continue
+            if name[0] != dim:
+                index.append(slice(None))
+            elif name == "z_lo":
+                index.append(lax.rem(spot, 2))
+            elif name == "z_hi":
+                index.append(lax.div(spot, 2))
+            else:
+                index.append(spot)
+        return ref.at[tuple(index)]
+
+    def ring_copy(c, s, k):
+        dim = ORDERS[c][s]
+        number = 9 * c + 3 * s + k - 1
+        return remote(
+            piece(c, s, ring_place(dim, k)), landed[c][s].at[k - 1],
+            ring_send.at[number], ring_recv.at[number], ring_peer(dim, k),
+        )
+
+    for c in range(3):
+        first, width = COLORS[c]
+        cols = slice(first, first + width)
+        core_copy(c).wait_recv()
+        for zl in range(2):
+            for x in range(4):
+                held[c][0][zl, x] = sym[core, zl, x, :, :, :, cols] + core_in[zl, x, :, :, :, cols]
+        for k in (2, 1, 3):
+            ring_copy(c, 0, k).start()
+    for s in range(3):
+        for c in range(3):
+            first, width = COLORS[c]
+            for k in (1, 3, 2):
+                ring_copy(c, s, k).wait_recv()
+            total = piece(c, s, ring_place(ORDERS[c][s], 0))[...]
+            for k in (1, 3, 2):
+                total = total + landed[c][s][k - 1]
+            if s < 2:
+                held[c][s + 1][...] = total
+                for k in (2, 1, 3):
+                    ring_copy(c, s + 1, k).start()
+            else:
+                for tile in range(width // 128):
+                    col = first + 128 * tile
+                    part = total[:, 128 * tile : 128 * tile + 128]
+                    if col < K:
+                        stiff_out[:, col : col + 128] = part
+                    else:
+                        mass_out[:, col - K : col - K + 128] = part
+    for c in range(3):
+        core_copy(c).wait_send()
+        for s in range(3):
+            for k in (1, 2, 3):
+                ring_copy(c, s, k).wait_send()
 
     @pl.loop(0, SX)
     def _(x):
@@ -389,6 +497,17 @@
         @pl.when(has(-dx, -dy))
         def _():
             zcopy(index, -dx, -dy).wait_send()
+
+
+def ring_buffers():
+    buffers = []
+    for (_, width), order in zip(COLORS, ORDERS):
+        for s in range(3):
+            left = [n for d, n in (("z", 2), ("x", 4), ("y", 4), ("z", 2)) if d in order[s:]]
+            after = [n for d, n in (("z", 2), ("x", 4), ("y", 4), ("z", 2)) if d in order[s + 1 :]]
+            buffers.append(pltpu.VMEM((*left, 4, width), F32))
+            buffers.append(pltpu.VMEM((3, *after, 4, width), F32))
+    return buffers
 
 
 def local_products(eigvecs, material):
@@ -401,9 +520,9 @@
     dma = pltpu.SemaphoreType.DMA
     return pl.pallas_call(
         local_kernel,
-        out_shape=jax.ShapeDtypeStruct((K, 2 * K), F32),
+        out_shape=[jax.ShapeDtypeStruct((4, K), F32)] * 2,
         in_specs=[pl.BlockSpec(memory_space=pl.ANY)] + [vmem] * 8,
-        out_specs=vmem,
+        out_specs=[vmem, vmem],
         scratch_shapes=[
             pltpu.VMEM((PX, PY, SZ, K), BF16),
             pltpu.VMEM((PY, SZ, K), BF16),
@@ -420,6 +539,10 @@
             pltpu.VMEM((SX * SY, K), BF16),
             dma((SX,)), dma((SX,)), dma((SX,)), dma((SX,)), dma((SX,)),
             dma((6,)), dma((6,)), dma((9,)), dma((9,)),
+            pltpu.VMEM((2, 2, 4, 4, 2, 4, 2 * K), F32),
+            pltpu.VMEM((2, 4, 4, 2, 4, 2 * K), F32),
+            *ring_buffers(),
+            dma((3,)), dma((3,)), dma((27,)), dma((27,)),
         ],
         compiler_params=pltpu.CompilerParams(
             collective_id=0, has_side_effects=True, vmem_limit_bytes=60 * 1024 * 1024
@@ -427,22 +550,8 @@
     )(eigvecs, material, *small)
 
 
-def split_up(x, dim, devices):
-    dims = x.shape
-    parts = x.reshape(*dims[:dim], devices, dims[dim] // devices, *dims[dim + 1 :])
-    return jnp.moveaxis(parts, dim, 0)
-
-
-def sum_at_owner(x, axis, dim):
-    devices = lax.axis_size(axis)
-    parts = lax.all_to_all(split_up(x, dim, devices), axis, 0, 0, tiled=True)
-    return jnp.sum(parts, axis=0)
-
-
 def per_device(eigvecs, material):
-    both = local_products(eigvecs, material)
-    summed = sum_at_owner(sum_at_owner(sum_at_owner(both, "gx", 0), "gy", 0), "gz", 0)
-    return summed[:, :K], summed[:, K:]
+    return tuple(local_products(eigvecs, material))
 
 
 def solution(mesh):

time: 102 us -> 66.1 us (0.65)
  blocking collectives: 56.8 us -> 0 us
  Pallas kernels: 43.3 us -> 62.7 us
  local copies, waits for them, and re-layouts: 0.62 us -> 2.59 us
    all_to_all x3 -> x0, blocking collectives: 56.8 us -> none  [sum_at_owner(): parts = lax.all_to_all(split_up(x, dim, devices), axis, 0, 0, tiled=True)]
    pallas_call x1, Pallas kernels: 43.3 us -> 62.7 us  [local_products(): pl.pallas_call(local_kernel, out_shape=[jax.ShapeDtypeStruct((4, K), F32)...]
    unnamed x0 -> x2, local copies, waits for them, and re-layouts: none -> 2.59 us
where the time goes in v2:
time: 66.1 us; the launch traced here: 65.9 us
  Pallas kernels  62.7 us (95%)
  local copies, waits for them, and re-layouts  2.59 us (4%)
    pallas_call x1, Pallas kernels, local_products(): pl.pallas_call(local_kernel, out_shape=[jax.ShapeDtypeStruct((4, K), F32)...  62.7 us
    unnamed x2, local copies, waits for them, and re-layouts  2.59 us

profile of v2, /device:TPU:0, one launch (start us, length us, event | category | flops | bytes accessed | tf_op | source)
XLA Modules:
  0.0 65.9 jit_solution(17006537883248985529)
XLA Ops:
  0.6 62.7 %shard_map.104 = (f32[4,512]{1,0:T(4,128)}, f32[4,512]{1,0:T(4,128)}) custom-call(bf16[16,8,48,512]{3,2,1,0:T(8,128)(2,1)} %v_hbm.1, f32[2,16,8,48]{3,2,1,0:T(8,128)} %mat.1, bf16[240,240]{1,0:T(8,128)(2,1)} %constant.14.clone.tz_ref, f32[128,256]{1,0:T(8,128)} %constant.15.clone.sel_ref, f32[128,256]{1,0:T(8,128)} %constant.16.clone.txy_ref, ...), custom_call_target="tpu_custom_call" | custom-call | tf_op jit(solution)/shard_map/pallas_call | solution.py:521
  63.3 1.3 %copy.13 = f32[4,512]{1,0:T(4,128)} copy(f32[4,512]{1,0:T(4,128)} %get-tuple-element.4) | data formatting | bytes 16384
  64.6 1.3 %copy.14 = f32[4,512]{1,0:T(4,128)} copy(f32[4,512]{1,0:T(4,128)} %get-tuple-element.5) | data formatting | bytes 16384

commit v3 on v2

--- a/solution.py
+++ b/solution.py
@@ -16,6 +16,7 @@
 SX, SY, SZ, K = 16, 8, 48, 512
 PX, PY = SX + 2, SY + 2
 HALF = PY // 2
+PAIR_ROWS = 2 * SY * SZ + 4 * SZ
 CELLS = 64 * 128 * 96
 DIM0 = (((0,), (0,)), ((), ()))
 COLORS = ((0, 384), (384, 384), (768, 256))
@@ -73,7 +74,7 @@
 
 def local_kernel(
     v_hbm, mat, tz_ref, sel_ref, txy_ref, t2_ref, t4_ref, t2t_ref, pick_ref, stiff_out, mass_out,
-    vp, az, bz, ya, yb, xbuf, vt, coef, acc, zf, zs, zh, zface,
+    vp, az, bz, ya, yb, xbufs, vts, xbuf, vt, coef, acc, zf, zs, zh, zface,
     own_sem, up_send, dn_send, up_recv, dn_recv, side_send, side_recv, z_send, z_recv,
     sym, core_in, *ring,
 ):
@@ -291,7 +292,6 @@
                     side(index).wait_recv()
 
     def plane_stage(xp, slot):
-        wait_plane(xp)
         for b in range(2):
             for c in range(2):
                 lanes = slice(256 * c, 256 * c + 256)
@@ -299,89 +299,131 @@
                 a = jnp.dot(
                     tz_ref[...], own.reshape(HALF * SZ, 256), preferred_element_type=F32
                 ).astype(BF16).reshape(HALF, SZ, 256)
-                az[HALF * b : HALF * b + HALF, :, lanes] = a
-                bz[HALF * b : HALF * b + HALF, :, lanes] = a + (own + own)
+                az[slot % 2][HALF * b : HALF * b + HALF, :, lanes] = a
+                bz[slot % 2][HALF * b : HALF * b + HALF, :, lanes] = a + (own + own)
+        for c in range(2):
+            lanes = slice(256 * c, 256 * c + 256)
+            a, b = az[slot % 2], bz[slot % 2]
+            pair = a[0, :, lanes] + a[1, :, lanes]
+            for y in range(SY):
+                nxt = a[y + 1, :, lanes] + a[y + 2, :, lanes]
+                ya[slot][y, :, lanes] = pair + nxt
+                pair = nxt
+                yb[slot][y, :, lanes] = (b[y, :, lanes] + b[y + 2, :, lanes]) + BF16(4.0) * b[y + 1, :, lanes]
+
+    def cell_pair(x, slot, side_by):
+        x_out, v_out = xbufs[side_by], vts[side_by]
+        slots = [(slot + i) % 4 for i in range(4)]
         for y in range(SY):
-            mid = az[y + 1]
-            ya[slot, y] = (az[y] + az[y + 2]) + (mid + mid)
-            mid = bz[y + 1]
-            yb[slot, y] = (bz[y] + bz[y + 2]) + BF16(4.0) * mid
-
-    def cell_stage(x):
-        s0, s1, s2 = lax.rem(x, 3), lax.rem(x + 1, 3), lax.rem(x + 2, 3)
-        for y in range(SY):
-            al = coef[x + 1, 0, :, y + 1 : y + 2]
-            be = coef[x + 1, 1, :, y + 1 : y + 2]
-            ro = coef[x + 1, 2, :, y + 1 : y + 2]
-            mid = ya[s1, y]
-            u = (ya[s0, y] + ya[s2, y]) + (mid + mid)
-            mid = yb[s1, y]
-            m = (yb[s0, y] + yb[s2, y]) + BF16(4.0) * mid
-            own = vp[x + 1, y + 1].astype(F32)
-            xbuf[pl.ds(y * SZ, SZ), 0:K] = (al * own - be * u.astype(F32)).astype(BF16)
-            xbuf[pl.ds(y * SZ, SZ), K : 2 * K] = (ro * m.astype(F32)).astype(BF16)
-        vt[...] = vp[x + 1, 1 : 1 + SY].reshape(SY * SZ, K).T
+            cols = [
+                [coef[x + 1 + i, n, :, y + 1 : y + 2] for n in range(3)] for i in range(2)
+            ]
+            for c in range(2):
+                lanes = slice(256 * c, 256 * c + 256)
+                stage = [ya[n][y, :, lanes] for n in slots]
+                sums = [stage[i] + stage[i + 1] for i in range(3)]
+                other_stage = [yb[n][y, :, lanes] for n in slots]
+                for i in range(2):
+                    al, be, ro = cols[i]
+                    row = pl.ds(SY * SZ * i + y * SZ, SZ)
+                    u = (sums[i] + sums[i + 1]).astype(F32)
+                    own = vp[x + 1 + i, y + 1, :, lanes].astype(F32)
+                    x_out[row, 256 * c : 256 * c + 256] = (al * own - be * u).astype(BF16)
+                    m = (other_stage[i] + other_stage[i + 2]) + BF16(4.0) * other_stage[i + 1]
+                    x_out[row, K + 256 * c : K + 256 * c + 256] = (ro * m.astype(F32)).astype(BF16)
+        for i in range(2):
+            for n, yp in enumerate((0, PY - 1)):
+                row = pl.ds(2 * SY * SZ + (2 * i + n) * SZ, SZ)
+                x_out[row, 0:K] = halo_rows(x + 1 + i, yp).astype(BF16)
+        for i in range(2):
+            v_out[:, SY * SZ * i : SY * SZ * i + SY * SZ] = (
+                vp[x + 1 + i, 1 : 1 + SY].reshape(SY * SZ, K).T
+            )
+        sides_of = jnp.concatenate([vp[x + 1 + i, yp] for i in range(2) for yp in (0, PY - 1)], axis=0)
+        v_out[:, 2 * SY * SZ : 2 * SY * SZ + 4 * SZ] = sides_of.T
+
+    def gram_pair(side_by):
+        x_in, v_in = xbufs[side_by], vts[side_by]
         for c in range(4):
             lanes = slice(256 * c, 256 * c + 256)
-            acc[:, lanes] += jnp.dot(vt[...], xbuf[:, lanes], preferred_element_type=F32)
-
-    plane_stage(jnp.int32(0), jnp.int32(0))
-    plane_stage(jnp.int32(1), jnp.int32(1))
-
-    @pl.loop(0, SX)
-    def _(x):
-        plane_stage(x + 2, lax.rem(x + 2, 3))
-        cell_stage(x)
+            depth = PAIR_ROWS if c < 2 else 2 * SY * SZ
+            acc[:, lanes] += jnp.dot(
+                v_in[:, 0:depth], x_in[0:depth, lanes], preferred_element_type=F32
+            )
 
     def halo_rows(xp, yp):
         return coef[xp, 0, :, yp : yp + 1] * vp[xp, yp].astype(F32)
 
-    for xp in (0, PX - 1):
-        for y in range(SY):
-            xbuf[y * SZ : y * SZ + SZ, 0:K] = halo_rows(xp, y + 1).astype(BF16)
-        vt[...] = vp[xp, 1 : 1 + SY].reshape(SY * SZ, K).T
-        for c in range(2):
-            lanes = slice(256 * c, 256 * c + 256)
-            acc[:, lanes] += jnp.dot(vt[...], xbuf[:, lanes], preferred_element_type=F32)
-    for yp in (0, PY - 1):
-        @pl.loop(0, 3)
-        def _(part):
-            for i in range(6):
-                xbuf[i * SZ : i * SZ + SZ, 0:K] = halo_rows(part * 6 + i, yp).astype(BF16)
-            turned = vp[pl.ds(part * 6, 6), yp].reshape(6 * SZ, K).T
+    def side_products():
+        for xp in (0, PX - 1):
+            for y in range(PY):
+                xbuf[y * SZ : y * SZ + SZ, 0:K] = halo_rows(xp, y).astype(BF16)
+            vt[...] = vp[xp].reshape(PY * SZ, K).T
             for c in range(2):
                 lanes = slice(256 * c, 256 * c + 256)
-                acc[:, lanes] += jnp.dot(turned, xbuf[0 : 6 * SZ, lanes], preferred_element_type=F32)
-
-    for index, (dx, dy, _, _) in enumerate(zrows):
-
-        @pl.when(has(dx, dy))
-        def _():
-            zcopy(index, -dx, -dy).wait_recv()
-
-    lane = lax.broadcasted_iota(jnp.int32, (SX * SY, SZ), 1)
-    at_edge = lane == jnp.where(gz == 0, SZ - 1, 0)
-    kappa_edge = jnp.sum(jnp.where(at_edge, kappa, 0.0), axis=1, keepdims=True)
-    rho_edge = jnp.sum(jnp.where(at_edge, rho, 0.0), axis=1, keepdims=True)
-    far = zh[...]
-    du = jnp.dot(t2_ref[...], far, preferred_element_type=F32)
-    dm = jnp.dot(t4_ref[...], far, preferred_element_type=F32)
-    xbuf[0:128, 0:K] = (kappa_edge * (-1.0 / 16.0) * du).astype(BF16)
-    xbuf[0:128, K : 2 * K] = (rho_edge * dm).astype(BF16)
-    turned = zface[...].T
-    for c in range(4):
-        lanes = slice(256 * c, 256 * c + 256)
-        acc[:, lanes] += jnp.dot(turned, xbuf[0:128, lanes], preferred_element_type=F32)
-    reach = jnp.dot(
-        t2t_ref[...], jnp.broadcast_to(kappa_edge, (128, 128)), precision=HIGH, preferred_element_type=F32
-    ) * (1.0 / 32.0)
-    for c in range(4):
-        lanes = slice(128 * c, 128 * c + 128)
-        xbuf[0:256, lanes] = (reach * far[:, lanes].astype(F32)).astype(BF16)
-    turned = far.T
-    for c in range(2):
-        lanes = slice(256 * c, 256 * c + 256)
-        acc[:, lanes] += jnp.dot(turned, xbuf[0:256, lanes], preferred_element_type=F32)
+                acc[:, lanes] += jnp.dot(vt[...], xbuf[:, lanes], preferred_element_type=F32)
+        for index, (dx, dy, _, _) in enumerate(zrows):
+
+            @pl.when(has(dx, dy))
+            def _():
+                zcopy(index, -dx, -dy).wait_recv()
+
+        lane = lax.broadcasted_iota(jnp.int32, (SX * SY, SZ), 1)
+        at_edge = lane == jnp.where(gz == 0, SZ - 1, 0)
+        kappa_edge = jnp.sum(
+            jnp.where(at_edge, mat[0].reshape(SX * SY, SZ), 0.0), axis=1, keepdims=True
+        )
+        rho_edge = jnp.sum(
+            jnp.where(at_edge, mat[1].reshape(SX * SY, SZ), 0.0), axis=1, keepdims=True
+        )
+        far = zh[...]
+        du = jnp.dot(t2_ref[...], far, preferred_element_type=F32)
+        dm = jnp.dot(t4_ref[...], far, preferred_element_type=F32)
+        xbuf[0:128, 0:K] = (kappa_edge * (-1.0 / 16.0) * du).astype(BF16)
+        xbuf[0:128, K : 2 * K] = (rho_edge * dm).astype(BF16)
+        reach = jnp.dot(
+            t2t_ref[...], jnp.broadcast_to(kappa_edge, (128, 128)), precision=HIGH, preferred_element_type=F32
+        ) * (1.0 / 32.0)
+        for c in range(4):
+            lanes = slice(128 * c, 128 * c + 128)
+            xbuf[128:384, lanes] = (reach * far[:, lanes].astype(F32)).astype(BF16)
+        vt[:, 0:128] = zface[...].T
+        vt[:, 128:384] = far.T
+        for c in range(4):
+            lanes = slice(256 * c, 256 * c + 256)
+            depth = 384 if c < 2 else 128
+            acc[:, lanes] += jnp.dot(vt[:, 0:depth], xbuf[0:depth, lanes], preferred_element_type=F32)
+
+    for ref in (xbufs[1], vts[1]):
+        ref[...] = jnp.zeros_like(ref)
+    for n in range(4):
+        wait_plane(jnp.int32(n))
+        plane_stage(n, n)
+
+    @pl.loop(0, 3)
+    def _(t):
+        x = 4 * t
+        for half in range(2):
+            for n in range(2):
+                wait_plane(x + 2 * half + 4 + n)
+            gram_pair(1 - half)
+            cell_pair(x + 2 * half, 2 * half, half)
+            for n in range(2):
+                plane_stage(x + 2 * half + 4 + n, 2 * half + n)
+
+        @pl.when(t == 1)
+        def _():
+            wait_plane(jnp.int32(PX - 1))
+            side_products()
+
+    wait_plane(jnp.int32(16))
+    gram_pair(1)
+    cell_pair(12, 0, 0)
+    for n in range(2):
+        plane_stage(16 + n, n)
+    gram_pair(0)
+    cell_pair(14, 2, 1)
+    gram_pair(1)
 
     def core_copy(c):
         first, width = COLORS[c]
@@ -525,12 +567,14 @@
         out_specs=[vmem, vmem],
         scratch_shapes=[
             pltpu.VMEM((PX, PY, SZ, K), BF16),
-            pltpu.VMEM((PY, SZ, K), BF16),
-            pltpu.VMEM((PY, SZ, K), BF16),
-            pltpu.VMEM((3, SY, SZ, K), BF16),
-            pltpu.VMEM((3, SY, SZ, K), BF16),
-            pltpu.VMEM((SY * SZ, 2 * K), BF16),
-            pltpu.VMEM((K, SY * SZ), BF16),
+            [pltpu.VMEM((PY, SZ, K), BF16)] * 2,
+            [pltpu.VMEM((PY, SZ, K), BF16)] * 2,
+            [pltpu.VMEM((SY, SZ, K), BF16)] * 4,
+            [pltpu.VMEM((SY, SZ, K), BF16)] * 4,
+            [pltpu.VMEM((PAIR_ROWS, 2 * K), BF16)] * 2,
+            [pltpu.VMEM((K, PAIR_ROWS), BF16)] * 2,
+            pltpu.VMEM((PY * SZ, 2 * K), BF16),
+            pltpu.VMEM((K, PY * SZ), BF16),
             pltpu.VMEM((PX, 3, SZ, 128), F32),
             pltpu.VMEM((K, 2 * K), F32),
             pltpu.VMEM((SX * SY, K), F32),

time: 66.1 us -> 63.1 us (0.955)
  Pallas kernels: 62.7 us -> 59.7 us
    pallas_call x1, Pallas kernels: 62.7 us -> 59.7 us  [local_products(): pl.pallas_call(local_kernel, out_shape=[jax.ShapeDtypeStruct((4, K), F32)...]
where the time goes in v3:
time: 63.1 us; the launch traced here: 62.9 us
  Pallas kernels  59.7 us (95%)
  local copies, waits for them, and re-layouts  2.59 us (4%)
  between operations  0.64 us (1%)
    pallas_call x1, Pallas kernels, local_products(): pl.pallas_call(local_kernel, out_shape=[jax.ShapeDtypeStruct((4, K), F32)...  59.7 us
    unnamed x2, local copies, waits for them, and re-layouts  2.59 us

profile of v3, /device:TPU:0, one launch (start us, length us, event | category | flops | bytes accessed | tf_op | source)
XLA Modules:
  0.0 62.9 jit_solution(17770226457340940173)
XLA Ops:
  0.6 59.7 %shard_map.104 = (f32[4,512]{1,0:T(4,128)}, f32[4,512]{1,0:T(4,128)}) custom-call(bf16[16,8,48,512]{3,2,1,0:T(8,128)(2,1)} %v_hbm.1, f32[2,16,8,48]{3,2,1,0:T(8,128)} %mat.1, bf16[240,240]{1,0:T(8,128)(2,1)} %constant.14.clone.tz_ref, f32[128,256]{1,0:T(8,128)} %constant.15.clone.sel_ref, f32[128,256]{1,0:T(8,128)} %constant.16.clone.txy_ref, ...), custom_call_target="tpu_custom_call" | custom-call | tf_op jit(solution)/shard_map/pallas_call | solution.py:563
  60.3 1.3 %copy.13 = f32[4,512]{1,0:T(4,128)} copy(f32[4,512]{1,0:T(4,128)} %get-tuple-element.4) | data formatting | bytes 16384
  61.6 1.3 %copy.14 = f32[4,512]{1,0:T(4,128)} copy(f32[4,512]{1,0:T(4,128)} %get-tuple-element.5) | data formatting | bytes 16384

commit v4 on v3

--- a/solution.py
+++ b/solution.py
@@ -73,7 +73,7 @@
 
 
 def local_kernel(
-    v_hbm, mat, tz_ref, sel_ref, txy_ref, t2_ref, t4_ref, t2t_ref, pick_ref, stiff_out, mass_out,
+    v_hbm, mat, tz_ref, sel_ref, txy_ref, t2_ref, t4_ref, t2t_ref, pick_ref, out,
     vp, az, bz, ya, yb, xbufs, vts, xbuf, vt, coef, acc, zf, zs, zh, zface,
     own_sem, up_send, dn_send, up_recv, dn_recv, side_send, side_recv, z_send, z_recv,
     sym, core_in, *ring,
@@ -151,11 +151,14 @@
         dst_x = 0 if dx == 1 else PX - 1
         if dy == 0:
             src, dst = v_hbm.at[src_x], vp.at[dst_x, pl.ds(1, SY)]
-        elif dy == 1:
-            src, dst = v_hbm.at[src_x, SY - 1], vp.at[dst_x, 0]
         else:
-            src, dst = v_hbm.at[src_x, 0], vp.at[dst_x, PY - 1]
-        return remote(src, dst, side_send.at[index], side_recv.at[index], at(dx, dy, gz))
+            row = 0 if dy == 1 else PY - 1
+            src, dst = vp.at[src_x + 1, row], vp.at[dst_x, row]
+        return remote(src, dst, side_send.at[index], side_recv.at[index], at(dx, 0, gz))
+
+    def side_sent(index):
+        dx, dy = sides[index]
+        return has(dx, -dy)
 
     sides = [(1, 0), (1, 1), (1, -1), (-1, 0), (-1, 1), (-1, -1)]
 
@@ -194,14 +197,7 @@
     def _():
         side(3).start()
 
-    for index in (1, 2, 4, 5):
-
-        @pl.when(has(*sides[index]))
-        def _():
-            side(index).start()
-
-    @pl.loop(0, SX)
-    def _(x):
+    def send_plane(x):
         @pl.when(has(0, 1))
         def _():
             up(x).start()
@@ -209,6 +205,10 @@
         @pl.when(has(0, -1))
         def _():
             down(x).start()
+
+    send_plane(SX - 1)
+    send_plane(0)
+    pl.loop(1, SX - 1)(send_plane)
 
     kappa = mat[0].reshape(SX * SY, SZ)
     rho = mat[1].reshape(SX * SY, SZ)
@@ -260,36 +260,32 @@
         def _():
             zcopy(index, -dx, -dy).start()
 
+    def wait_rows(x):
+        @pl.when(has(0, -1))
+        def _():
+            up(x).wait_recv()
+
+        @pl.when(has(0, 1))
+        def _():
+            down(x).wait_recv()
+
+    wait_rows(SX - 1)
+    wait_rows(0)
+    for index in (1, 2, 4, 5):
+
+        @pl.when(side_sent(index))
+        def _():
+            side(index).start()
+
     acc[...] = jnp.zeros_like(acc)
 
-    def wait_plane(xp):
-        @pl.when(jnp.logical_and(xp >= 1, xp <= SX))
-        def _():
-            @pl.when(has(0, -1))
+    def wait_sides(group):
+        for index in group:
+            dx, dy = sides[index]
+
+            @pl.when(has(-dx, -dy))
             def _():
-                up(xp - 1).wait_recv()
-
-            @pl.when(has(0, 1))
-            def _():
-                down(xp - 1).wait_recv()
-
-        @pl.when(xp == 0)
-        def _():
-            for index in (0, 1, 2):
-                dx, dy = sides[index]
-
-                @pl.when(has(-dx, -dy))
-                def _():
-                    side(index).wait_recv()
-
-        @pl.when(xp == PX - 1)
-        def _():
-            for index in (3, 4, 5):
-                dx, dy = sides[index]
-
-                @pl.when(has(-dx, -dy))
-                def _():
-                    side(index).wait_recv()
+                side(index).wait_recv()
 
     def plane_stage(xp, slot):
         for b in range(2):
@@ -311,9 +307,8 @@
                 pair = nxt
                 yb[slot][y, :, lanes] = (b[y, :, lanes] + b[y + 2, :, lanes]) + BF16(4.0) * b[y + 1, :, lanes]
 
-    def cell_pair(x, slot, side_by):
+    def cell_pair(x, slots, side_by):
         x_out, v_out = xbufs[side_by], vts[side_by]
-        slots = [(slot + i) % 4 for i in range(4)]
         for y in range(SY):
             cols = [
                 [coef[x + 1 + i, n, :, y + 1 : y + 2] for n in range(3)] for i in range(2)
@@ -396,33 +391,35 @@
 
     for ref in (xbufs[1], vts[1]):
         ref[...] = jnp.zeros_like(ref)
-    for n in range(4):
-        wait_plane(jnp.int32(n))
+    plane_stage(1, 1)
+    for n in (2, 3):
+        wait_rows(n - 1)
         plane_stage(n, n)
+    wait_sides((0, 1, 2))
+    plane_stage(0, 0)
 
     @pl.loop(0, 3)
     def _(t):
         x = 4 * t
         for half in range(2):
+            gram_pair(1 - half)
+            cell_pair(x + 2 * half, (0, 1, 2, 3) if half == 0 else (2, 3, 0, 1), half)
             for n in range(2):
-                wait_plane(x + 2 * half + 4 + n)
-            gram_pair(1 - half)
-            cell_pair(x + 2 * half, 2 * half, half)
+                wait_rows(x + 2 * half + 3 + n)
             for n in range(2):
                 plane_stage(x + 2 * half + 4 + n, 2 * half + n)
 
         @pl.when(t == 1)
         def _():
-            wait_plane(jnp.int32(PX - 1))
+            wait_sides((3, 4, 5))
             side_products()
-
-    wait_plane(jnp.int32(16))
+            plane_stage(SX, 4)
+            plane_stage(SX + 1, 5)
+
     gram_pair(1)
-    cell_pair(12, 0, 0)
-    for n in range(2):
-        plane_stage(16 + n, n)
+    cell_pair(12, (0, 1, 2, 3), 0)
     gram_pair(0)
-    cell_pair(14, 2, 1)
+    cell_pair(14, (2, 3, 4, 5), 1)
     gram_pair(1)
 
     def core_copy(c):
@@ -508,10 +505,7 @@
                 for tile in range(width // 128):
                     col = first + 128 * tile
                     part = total[:, 128 * tile : 128 * tile + 128]
-                    if col < K:
-                        stiff_out[:, col : col + 128] = part
-                    else:
-                        mass_out[:, col - K : col - K + 128] = part
+                    out[:, col : col + 128] = part
     for c in range(3):
         core_copy(c).wait_send()
         for s in range(3):
@@ -530,7 +524,7 @@
 
     for index in range(6):
 
-        @pl.when(has(*sides[index]))
+        @pl.when(side_sent(index))
         def _():
             side(index).wait_send()
 
@@ -562,15 +556,15 @@
     dma = pltpu.SemaphoreType.DMA
     return pl.pallas_call(
         local_kernel,
-        out_shape=[jax.ShapeDtypeStruct((4, K), F32)] * 2,
+        out_shape=jax.ShapeDtypeStruct((4, 2 * K), F32),
         in_specs=[pl.BlockSpec(memory_space=pl.ANY)] + [vmem] * 8,
-        out_specs=[vmem, vmem],
+        out_specs=vmem,
         scratch_shapes=[
             pltpu.VMEM((PX, PY, SZ, K), BF16),
             [pltpu.VMEM((PY, SZ, K), BF16)] * 2,
             [pltpu.VMEM((PY, SZ, K), BF16)] * 2,
-            [pltpu.VMEM((SY, SZ, K), BF16)] * 4,
-            [pltpu.VMEM((SY, SZ, K), BF16)] * 4,
+            [pltpu.VMEM((SY, SZ, K), BF16)] * 6,
+            [pltpu.VMEM((SY, SZ, K), BF16)] * 6,
             [pltpu.VMEM((PAIR_ROWS, 2 * K), BF16)] * 2,
             [pltpu.VMEM((K, PAIR_ROWS), BF16)] * 2,
             pltpu.VMEM((PY * SZ, 2 * K), BF16),
@@ -595,7 +589,8 @@
 
 
 def per_device(eigvecs, material):
-    return tuple(local_products(eigvecs, material))
+    both = local_products(eigvecs, material)
+    return both[:, :K], both[:, K:]
 
 
 def solution(mesh):

time: 63.1 us -> 60.4 us (0.957)
  Pallas kernels: 59.7 us -> 58.2 us
  local copies, waits for them, and re-layouts: 2.59 us -> 1.32 us
    unnamed x2 -> x0, local copies, waits for them, and re-layouts: 2.59 us -> none
    pallas_call x1, Pallas kernels: 59.7 us -> 58.2 us  [local_products(): pl.pallas_call(local_kernel, out_shape=jax.ShapeDtypeStruct((4, 2 * K), F...]
    slice x0 -> x1, local copies, waits for them, and re-layouts: none -> 1.32 us  [per_device(): return (both[:, :K], both[:, K:])]
where the time goes in v4:
time: 60.4 us; the launch traced here: 60.2 us
  Pallas kernels  58.2 us (96%)
  local copies, waits for them, and re-layouts  1.32 us (2%)
  between operations  0.64 us (1%)
    pallas_call x1, Pallas kernels, local_products(): pl.pallas_call(local_kernel, out_shape=jax.ShapeDtypeStruct((4, 2 * K), F...  58.2 us
    slice x1, local copies, waits for them, and re-layouts, per_device(): return (both[:, :K], both[:, K:])  1.32 us

profile of v4, /device:TPU:0, one launch (start us, length us, event | category | flops | bytes accessed | tf_op | source)
XLA Modules:
  0.0 60.2 jit_solution(14644693470356529640)
XLA Ops:
  0.6 58.2 %shard_map.104 = f32[4,1024]{1,0:T(4,128)} custom-call(bf16[16,8,48,512]{3,2,1,0:T(8,128)(2,1)} %v_hbm.1, f32[2,16,8,48]{3,2,1,0:T(8,128)} %mat.1, bf16[240,240]{1,0:T(8,128)(2,1)} %constant.14.clone.tz_ref, f32[128,256]{1,0:T(8,128)} %constant.15.clone.sel_ref, f32[128,256]{1,0:T(8,128)} %constant.16.clone.txy_ref, bf16[128,256]{1,0:T(8,128)(2,1)} %constant.17.clone.t2_ref, ...), custom_call_target="tpu_custom_call" | custom-call | tf_op jit(solution)/shard_map/pallas_call | solution.py:557
  58.9 1.3 %fusion = (f32[4,512]{1,0:T(4,128)}, f32[4,512]{1,0:T(4,128)}) fusion(f32[4,1024]{1,0:T(4,128)} %shard_map.104), kind=kLoop, calls=%fused_computation | loop fusion | bytes 32768 | tf_op jit(solution)/shard_map/slice | solution.py:593

commit v5 on v4

--- a/solution.py
+++ b/solution.py
@@ -208,7 +208,7 @@
 
     send_plane(SX - 1)
     send_plane(0)
-    pl.loop(1, SX - 1)(send_plane)
+    pl.loop(1, 7)(send_plane)
 
     kappa = mat[0].reshape(SX * SY, SZ)
     rho = mat[1].reshape(SX * SY, SZ)
@@ -259,6 +259,8 @@
         @pl.when(has(-dx, -dy))
         def _():
             zcopy(index, -dx, -dy).start()
+
+    pl.loop(7, SX - 1)(send_plane)
 
     def wait_rows(x):
         @pl.when(has(0, -1))
@@ -337,11 +339,11 @@
         sides_of = jnp.concatenate([vp[x + 1 + i, yp] for i in range(2) for yp in (0, PY - 1)], axis=0)
         v_out[:, 2 * SY * SZ : 2 * SY * SZ + 4 * SZ] = sides_of.T
 
-    def gram_pair(side_by):
+    def gram_pair(side_by, halves=(0, 1)):
         x_in, v_in = xbufs[side_by], vts[side_by]
-        for c in range(4):
-            lanes = slice(256 * c, 256 * c + 256)
-            depth = PAIR_ROWS if c < 2 else 2 * SY * SZ
+        for c in halves:
+            lanes = slice(K * c, K * c + K)
+            depth = 2 * SY * SZ if c else PAIR_ROWS
             acc[:, lanes] += jnp.dot(
                 v_in[:, 0:depth], x_in[0:depth, lanes], preferred_element_type=F32
             )
@@ -420,7 +422,6 @@
     cell_pair(12, (0, 1, 2, 3), 0)
     gram_pair(0)
     cell_pair(14, (2, 3, 4, 5), 1)
-    gram_pair(1)
 
     def core_copy(c):
         first, width = COLORS[c]
@@ -437,6 +438,7 @@
             ] = block[4 * part : 4 * part + 4]
 
     for half, scale in ((0, 0.5 / CELLS), (1, 0.5 / (216.0 * CELLS))):
+        gram_pair(1, (half,))
         for i in range(4):
             for j in range(i, 4):
                 rows = slice(128 * i, 128 * i + 128)

time: 60.4 us -> 58.2 us (0.964)
  Pallas kernels: 58.2 us -> 56.1 us
    pallas_call x1, Pallas kernels: 58.2 us -> 56.1 us  [local_products(): pl.pallas_call(local_kernel, out_shape=jax.ShapeDtypeStruct((4, 2 * K), F...]
where the time goes in v5:
time: 58.2 us; the launch traced here: 58 us
  Pallas kernels  56.1 us (96%)
  local copies, waits for them, and re-layouts  1.32 us (2%)
  between operations  0.64 us (1%)
    pallas_call x1, Pallas kernels, local_products(): pl.pallas_call(local_kernel, out_shape=jax.ShapeDtypeStruct((4, 2 * K), F...  56.1 us
    slice x1, local copies, waits for them, and re-layouts, per_device(): return (both[:, :K], both[:, K:])  1.32 us

profile of v5, /device:TPU:0, one launch (start us, length us, event | category | flops | bytes accessed | tf_op | source)
XLA Modules:
  0.0 58.0 jit_solution(4957362871899124271)
XLA Ops:
  0.6 56.1 %shard_map.104 = f32[4,1024]{1,0:T(4,128)} custom-call(bf16[16,8,48,512]{3,2,1,0:T(8,128)(2,1)} %v_hbm.1, f32[2,16,8,48]{3,2,1,0:T(8,128)} %mat.1, bf16[240,240]{1,0:T(8,128)(2,1)} %constant.14.clone.tz_ref, f32[128,256]{1,0:T(8,128)} %constant.15.clone.sel_ref, f32[128,256]{1,0:T(8,128)} %constant.16.clone.txy_ref, bf16[128,256]{1,0:T(8,128)(2,1)} %constant.17.clone.t2_ref, ...), custom_call_target="tpu_custom_call" | custom-call | tf_op jit(solution)/shard_map/pallas_call | solution.py:559
  56.7 1.3 %fusion = (f32[4,512]{1,0:T(4,128)}, f32[4,512]{1,0:T(4,128)}) fusion(f32[4,1024]{1,0:T(4,128)} %shard_map.104), kind=kLoop, calls=%fused_computation | loop fusion | bytes 32768 | tf_op jit(solution)/shard_map/slice | solution.py:595

commit v6 on v5

--- a/solution.py
+++ b/solution.py
@@ -76,6 +76,7 @@
     v_hbm, mat, tz_ref, sel_ref, txy_ref, t2_ref, t4_ref, t2t_ref, pick_ref, out,
     vp, az, bz, ya, yb, xbufs, vts, xbuf, vt, coef, acc, zf, zs, zh, zface,
     own_sem, up_send, dn_send, up_recv, dn_recv, side_send, side_recv, z_send, z_recv,
+    face_send, face_recv, zpiece_send, zpiece_recv,
     sym, core_in, *ring,
 ):
     core_send, core_recv, ring_send, ring_recv = ring[-4:]
@@ -147,20 +148,25 @@
 
     def side(index):
         dx, dy = sides[index]
-        src_x = SX - 1 if dx == 1 else 0
+        src_x = SX if dx == 1 else 1
         dst_x = 0 if dx == 1 else PX - 1
-        if dy == 0:
-            src, dst = v_hbm.at[src_x], vp.at[dst_x, pl.ds(1, SY)]
-        else:
-            row = 0 if dy == 1 else PY - 1
-            src, dst = vp.at[src_x + 1, row], vp.at[dst_x, row]
-        return remote(src, dst, side_send.at[index], side_recv.at[index], at(dx, 0, gz))
+        row = 0 if dy == 1 else PY - 1
+        return remote(
+            vp.at[src_x, row], vp.at[dst_x, row], side_send.at[index], side_recv.at[index], at(dx, 0, gz)
+        )
+
+    def face(dx, row):
+        index = 0 if dx == 1 else 1
+        return remote(
+            v_hbm.at[SX - 1 if dx == 1 else 0, row], vp.at[0 if dx == 1 else PX - 1, row + 1],
+            face_send.at[index, row], face_recv.at[index, row], at(dx, 0, gz),
+        )
 
     def side_sent(index):
         dx, dy = sides[index]
         return has(dx, -dy)
 
-    sides = [(1, 0), (1, 1), (1, -1), (-1, 0), (-1, 1), (-1, -1)]
+    sides = [(1, 1), (1, -1), (-1, 1), (-1, -1)]
 
     @pl.when(jnp.logical_not(has(0, -1)))
     def _():
@@ -189,14 +195,6 @@
 
     pl.semaphore_wait(barrier, 27)
 
-    @pl.when(has(1, 0))
-    def _():
-        side(0).start()
-
-    @pl.when(has(-1, 0))
-    def _():
-        side(3).start()
-
     def send_plane(x):
         @pl.when(has(0, 1))
         def _():
@@ -206,9 +204,16 @@
         def _():
             down(x).start()
 
-    send_plane(SX - 1)
-    send_plane(0)
-    pl.loop(1, 7)(send_plane)
+    for n, x in enumerate((SX - 1, 0, 1, 2)):
+        send_plane(x)
+        for dx in (1, -1):
+
+            @pl.when(has(dx, 0))
+            def _():
+                face(dx, 2 * n).start()
+                face(dx, 2 * n + 1).start()
+
+    pl.loop(3, 6)(send_plane)
 
     kappa = mat[0].reshape(SX * SY, SZ)
     rho = mat[1].reshape(SX * SY, SZ)
@@ -254,13 +259,22 @@
             src, zh.at[pl.ds(first, count)], z_send.at[index], z_recv.at[index], at(dx, dy, other)
         )
 
-    for index, (dx, dy, _, _) in enumerate(zrows):
+    def zpiece(n):
+        rows = pl.ds(16 * n, 16)
+        return remote(
+            zface.at[rows], zh.at[rows], zpiece_send.at[n], zpiece_recv.at[n], at(0, 0, other)
+        )
+
+    for n in range(8):
+        zpiece(n).start()
+        dx, dy = zrows[n + 1][:2]
 
         @pl.when(has(-dx, -dy))
         def _():
-            zcopy(index, -dx, -dy).start()
-
-    pl.loop(7, SX - 1)(send_plane)
+            zcopy(n + 1, -dx, -dy).start()
+
+        send_plane(6 + n)
+    send_plane(SX - 2)
 
     def wait_rows(x):
         @pl.when(has(0, -1))
@@ -273,7 +287,7 @@
 
     wait_rows(SX - 1)
     wait_rows(0)
-    for index in (1, 2, 4, 5):
+    for index in range(4):
 
         @pl.when(side_sent(index))
         def _():
@@ -281,8 +295,13 @@
 
     acc[...] = jnp.zeros_like(acc)
 
-    def wait_sides(group):
-        for index in group:
+    def wait_sides(toward):
+        @pl.when(has(-toward, 0))
+        def _():
+            for row in range(SY):
+                face(toward, row).wait_recv()
+
+        for index in (0, 1) if toward == 1 else (2, 3):
             dx, dy = sides[index]
 
             @pl.when(has(-dx, -dy))
@@ -359,11 +378,14 @@
             for c in range(2):
                 lanes = slice(256 * c, 256 * c + 256)
                 acc[:, lanes] += jnp.dot(vt[...], xbuf[:, lanes], preferred_element_type=F32)
-        for index, (dx, dy, _, _) in enumerate(zrows):
+    def z_products():
+        for n in range(8):
+            zpiece(n).wait_recv()
+            dx, dy = zrows[n + 1][:2]
 
             @pl.when(has(dx, dy))
             def _():
-                zcopy(index, -dx, -dy).wait_recv()
+                zcopy(n + 1, -dx, -dy).wait_recv()
 
         lane = lax.broadcasted_iota(jnp.int32, (SX * SY, SZ), 1)
         at_edge = lane == jnp.where(gz == 0, SZ - 1, 0)
@@ -397,7 +419,7 @@
     for n in (2, 3):
         wait_rows(n - 1)
         plane_stage(n, n)
-    wait_sides((0, 1, 2))
+    wait_sides(1)
     plane_stage(0, 0)
 
     @pl.loop(0, 3)
@@ -413,11 +435,12 @@
 
         @pl.when(t == 1)
         def _():
-            wait_sides((3, 4, 5))
+            wait_sides(-1)
             side_products()
             plane_stage(SX, 4)
             plane_stage(SX + 1, 5)
 
+    z_products()
     gram_pair(1)
     cell_pair(12, (0, 1, 2, 3), 0)
     gram_pair(0)
@@ -474,13 +497,20 @@
                 index.append(spot)
         return ref.at[tuple(index)]
 
-    def ring_copy(c, s, k):
+    def ring_copies(c, s, ks):
         dim = ORDERS[c][s]
-        number = 9 * c + 3 * s + k - 1
-        return remote(
-            piece(c, s, ring_place(dim, k)), landed[c][s].at[k - 1],
-            ring_send.at[number], ring_recv.at[number], ring_peer(dim, k),
-        )
+        copies = []
+        for part in range(2 if s == 0 else 1):
+            for k in ks:
+                src, dst = piece(c, s, ring_place(dim, k)), landed[c][s].at[k - 1]
+                if s == 0:
+                    rows = pl.ds(part * (dst.shape[0] // 2), dst.shape[0] // 2)
+                    src, dst = src.at[rows], dst.at[rows]
+                number = 12 * c + (6 * part + k - 1 if s == 0 else 3 + 6 * (s - 1) + k - 1)
+                copies.append(
+                    remote(src, dst, ring_send.at[number], ring_recv.at[number], ring_peer(dim, k))
+                )
+        return copies
 
     for c in range(3):
         first, width = COLORS[c]
@@ -489,20 +519,20 @@
         for zl in range(2):
             for x in range(4):
                 held[c][0][zl, x] = sym[core, zl, x, :, :, :, cols] + core_in[zl, x, :, :, :, cols]
-        for k in (2, 1, 3):
-            ring_copy(c, 0, k).start()
+        for copy in ring_copies(c, 0, (2, 1, 3)):
+            copy.start()
     for s in range(3):
         for c in range(3):
             first, width = COLORS[c]
-            for k in (1, 3, 2):
-                ring_copy(c, s, k).wait_recv()
+            for copy in ring_copies(c, s, (1, 3, 2)):
+                copy.wait_recv()
             total = piece(c, s, ring_place(ORDERS[c][s], 0))[...]
             for k in (1, 3, 2):
                 total = total + landed[c][s][k - 1]
             if s < 2:
                 held[c][s + 1][...] = total
-                for k in (2, 1, 3):
-                    ring_copy(c, s + 1, k).start()
+                for copy in ring_copies(c, s + 1, (2, 1, 3)):
+                    copy.start()
             else:
                 for tile in range(width // 128):
                     col = first + 128 * tile
@@ -511,8 +541,8 @@
     for c in range(3):
         core_copy(c).wait_send()
         for s in range(3):
-            for k in (1, 2, 3):
-                ring_copy(c, s, k).wait_send()
+            for copy in ring_copies(c, s, (1, 2, 3)):
+                copy.wait_send()
 
     @pl.loop(0, SX)
     def _(x):
@@ -524,17 +554,26 @@
         def _():
             down(x).wait_send()
 
-    for index in range(6):
+    for index in range(4):
 
         @pl.when(side_sent(index))
         def _():
             side(index).wait_send()
 
-    for index, (dx, dy, _, _) in enumerate(zrows):
+    for dx in (1, -1):
+
+        @pl.when(has(dx, 0))
+        def _():
+            for row in range(SY):
+                face(dx, row).wait_send()
+
+    for n in range(8):
+        zpiece(n).wait_send()
+        dx, dy = zrows[n + 1][:2]
 
         @pl.when(has(-dx, -dy))
         def _():
-            zcopy(index, -dx, -dy).wait_send()
+            zcopy(n + 1, -dx, -dy).wait_send()
 
 
 def ring_buffers():
@@ -578,11 +617,12 @@
             pltpu.VMEM((256, K), BF16),
             pltpu.VMEM((SX * SY, K), BF16),
             dma((SX,)), dma((SX,)), dma((SX,)), dma((SX,)), dma((SX,)),
-            dma((6,)), dma((6,)), dma((9,)), dma((9,)),
+            dma((4,)), dma((4,)), dma((9,)), dma((9,)),
+            dma((2, SY)), dma((2, SY)), dma((8,)), dma((8,)),
             pltpu.VMEM((2, 2, 4, 4, 2, 4, 2 * K), F32),
             pltpu.VMEM((2, 4, 4, 2, 4, 2 * K), F32),
             *ring_buffers(),
-            dma((3,)), dma((3,)), dma((27,)), dma((27,)),
+            dma((3,)), dma((3,)), dma((36,)), dma((36,)),
         ],
         compiler_params=pltpu.CompilerParams(
             collective_id=0, has_side_effects=True, vmem_limit_bytes=60 * 1024 * 1024

time: 58.2 us -> 58.6 us (level)
  no operation moved by 1% of the time
where the time goes in v6:
time: 58.6 us; the launch traced here: 58.5 us
  Pallas kernels  56.5 us (96%)
  local copies, waits for them, and re-layouts  1.32 us (2%)
  between operations  0.64 us (1%)
    pallas_call x1, Pallas kernels, local_products(): pl.pallas_call(local_kernel, out_shape=jax.ShapeDtypeStruct((4, 2 * K), F...  56.5 us
    slice x1, local copies, waits for them, and re-layouts, per_device(): return (both[:, :K], both[:, K:])  1.32 us

profile of v6, /device:TPU:0, one launch (start us, length us, event | category | flops | bytes accessed | tf_op | source)
XLA Modules:
  0.0 58.5 jit_solution(14666553482307233950)
XLA Ops:
  0.6 56.5 %shard_map.104 = f32[4,1024]{1,0:T(4,128)} custom-call(bf16[16,8,48,512]{3,2,1,0:T(8,128)(2,1)} %v_hbm.1, f32[2,16,8,48]{3,2,1,0:T(8,128)} %mat.1, bf16[240,240]{1,0:T(8,128)(2,1)} %constant.14.clone.tz_ref, f32[128,256]{1,0:T(8,128)} %constant.15.clone.sel_ref, f32[128,256]{1,0:T(8,128)} %constant.16.clone.txy_ref, bf16[128,256]{1,0:T(8,128)(2,1)} %constant.17.clone.t2_ref, ...), custom_call_target="tpu_custom_call" | custom-call | tf_op jit(solution)/shard_map/pallas_call | solution.py:598
  57.2 1.3 %fusion = (f32[4,512]{1,0:T(4,128)}, f32[4,512]{1,0:T(4,128)}) fusion(f32[4,1024]{1,0:T(4,128)} %shard_map.104), kind=kLoop, calls=%fused_computation | loop fusion | bytes 32768 | tf_op jit(solution)/shard_map/slice | solution.py:635

commit v7 on v6

--- a/solution.py
+++ b/solution.py
@@ -213,7 +213,7 @@
                 face(dx, 2 * n).start()
                 face(dx, 2 * n + 1).start()
 
-    pl.loop(3, 6)(send_plane)
+    send_plane(3)
 
     kappa = mat[0].reshape(SX * SY, SZ)
     rho = mat[1].reshape(SX * SY, SZ)
@@ -234,6 +234,26 @@
         coef[xp, 1, :, 0:PY] = beta[:, span]
         coef[xp, 2, :, 0:PY] = own_rho[:, span]
 
+    def wait_rows(x):
+        @pl.when(has(0, -1))
+        def _():
+            up(x).wait_recv()
+
+        @pl.when(has(0, 1))
+        def _():
+            down(x).wait_recv()
+
+    wait_rows(SX - 1)
+    wait_rows(0)
+    for index in range(4):
+
+        @pl.when(side_sent(index))
+        def _():
+            side(index).start()
+
+    send_plane(4)
+    send_plane(5)
+
     @pl.loop(0, SX)
     def _(x):
         own_copy(x).wait()
@@ -275,23 +295,6 @@
 
         send_plane(6 + n)
     send_plane(SX - 2)
-
-    def wait_rows(x):
-        @pl.when(has(0, -1))
-        def _():
-            up(x).wait_recv()
-
-        @pl.when(has(0, 1))
-        def _():
-            down(x).wait_recv()
-
-    wait_rows(SX - 1)
-    wait_rows(0)
-    for index in range(4):
-
-        @pl.when(side_sent(index))
-        def _():
-            side(index).start()
 
     acc[...] = jnp.zeros_like(acc)
 

time: 58.6 us -> 57.2 us (0.976)
  Pallas kernels: 56.5 us -> 55 us
    pallas_call x1, Pallas kernels: 56.5 us -> 55 us  [local_products(): pl.pallas_call(local_kernel, out_shape=jax.ShapeDtypeStruct((4, 2 * K), F...]
where the time goes in v7:
time: 57.2 us; the launch traced here: 57 us
  Pallas kernels  55 us (96%)
  local copies, waits for them, and re-layouts  1.32 us (2%)
  between operations  0.64 us (1%)
    pallas_call x1, Pallas kernels, local_products(): pl.pallas_call(local_kernel, out_shape=jax.ShapeDtypeStruct((4, 2 * K), F...  55 us
    slice x1, local copies, waits for them, and re-layouts, per_device(): return (both[:, :K], both[:, K:])  1.32 us

profile of v7, /device:TPU:0, one launch (start us, length us, event | category | flops | bytes accessed | tf_op | source)
XLA Modules:
  0.0 57.0 jit_solution(434775784964925390)
XLA Ops:
  0.6 55.0 %shard_map.104 = f32[4,1024]{1,0:T(4,128)} custom-call(bf16[16,8,48,512]{3,2,1,0:T(8,128)(2,1)} %v_hbm.1, f32[2,16,8,48]{3,2,1,0:T(8,128)} %mat.1, bf16[240,240]{1,0:T(8,128)(2,1)} %constant.14.clone.tz_ref, f32[128,256]{1,0:T(8,128)} %constant.15.clone.sel_ref, f32[128,256]{1,0:T(8,128)} %constant.16.clone.txy_ref, bf16[128,256]{1,0:T(8,128)(2,1)} %constant.17.clone.t2_ref, ...), custom_call_target="tpu_custom_call" | custom-call | tf_op jit(solution)/shard_map/pallas_call | solution.py:601
  55.7 1.3 %fusion = (f32[4,512]{1,0:T(4,128)}, f32[4,512]{1,0:T(4,128)}) fusion(f32[4,1024]{1,0:T(4,128)} %shard_map.104), kind=kLoop, calls=%fused_computation | loop fusion | bytes 32768 | tf_op jit(solution)/shard_map/slice | solution.py:638

commit v8 on v7

--- a/solution.py
+++ b/solution.py
@@ -424,6 +424,10 @@
         plane_stage(n, n)
     wait_sides(1)
     plane_stage(0, 0)
+    wait_sides(-1)
+    plane_stage(SX, 4)
+    plane_stage(SX + 1, 5)
+    side_products()
 
     @pl.loop(0, 3)
     def _(t):
@@ -435,13 +439,6 @@
                 wait_rows(x + 2 * half + 3 + n)
             for n in range(2):
                 plane_stage(x + 2 * half + 4 + n, 2 * half + n)
-
-        @pl.when(t == 1)
-        def _():
-            wait_sides(-1)
-            side_products()
-            plane_stage(SX, 4)
-            plane_stage(SX + 1, 5)
 
     z_products()
     gram_pair(1)

time: 57.2 us -> 58.2 us (1.017)
  Pallas kernels: 55 us -> 56.1 us
    pallas_call x1, Pallas kernels: 55 us -> 56.1 us  [local_products(): pl.pallas_call(local_kernel, out_shape=jax.ShapeDtypeStruct((4, 2 * K), F...]
where the time goes in v8:
time: 58.2 us; the launch traced here: 58 us
  Pallas kernels  56.1 us (96%)
  local copies, waits for them, and re-layouts  1.32 us (2%)
  between operations  0.64 us (1%)
    pallas_call x1, Pallas kernels, local_products(): pl.pallas_call(local_kernel, out_shape=jax.ShapeDtypeStruct((4, 2 * K), F...  56.1 us
    slice x1, local copies, waits for them, and re-layouts, per_device(): return (both[:, :K], both[:, K:])  1.32 us

profile of v8, /device:TPU:0, one launch (start us, length us, event | category | flops | bytes accessed | tf_op | source)
XLA Modules:
  0.0 58.0 jit_solution(10390913689942186858)
XLA Ops:
  0.6 56.1 %shard_map.104 = f32[4,1024]{1,0:T(4,128)} custom-call(bf16[16,8,48,512]{3,2,1,0:T(8,128)(2,1)} %v_hbm.1, f32[2,16,8,48]{3,2,1,0:T(8,128)} %mat.1, bf16[240,240]{1,0:T(8,128)(2,1)} %constant.14.clone.tz_ref, f32[128,256]{1,0:T(8,128)} %constant.15.clone.sel_ref, f32[128,256]{1,0:T(8,128)} %constant.16.clone.txy_ref, bf16[128,256]{1,0:T(8,128)(2,1)} %constant.17.clone.t2_ref, ...), custom_call_target="tpu_custom_call" | custom-call | tf_op jit(solution)/shard_map/pallas_call | solution.py:598
  56.7 1.3 %fusion = (f32[4,512]{1,0:T(4,128)}, f32[4,512]{1,0:T(4,128)}) fusion(f32[4,1024]{1,0:T(4,128)} %shard_map.104), kind=kLoop, calls=%fused_computation | loop fusion | bytes 32768 | tf_op jit(solution)/shard_map/slice | solution.py:635

commit v9 on v7

--- a/solution.py
+++ b/solution.py
@@ -20,7 +20,7 @@
 CELLS = 64 * 128 * 96
 DIM0 = (((0,), (0,)), ((), ()))
 COLORS = ((0, 384), (384, 384), (768, 256))
-ORDERS = ("xyz", "yzx", "zxy")
+ORDERS = ("zxy", "xyz", "yzx")
 
 
 def constants():
@@ -436,7 +436,7 @@
             for n in range(2):
                 plane_stage(x + 2 * half + 4 + n, 2 * half + n)
 
-        @pl.when(t == 1)
+        @pl.when(t == 0)
         def _():
             wait_sides(-1)
             side_products()

time: 57.2 us -> 56.8 us (level)
  no operation moved by 1% of the time
where the time goes in v9:
time: 56.8 us; the launch traced here: 56.6 us
  Pallas kernels  54.7 us (96%)
  local copies, waits for them, and re-layouts  1.32 us (2%)
  between operations  0.64 us (1%)
    pallas_call x1, Pallas kernels, local_products(): pl.pallas_call(local_kernel, out_shape=jax.ShapeDtypeStruct((4, 2 * K), F...  54.7 us
    slice x1, local copies, waits for them, and re-layouts, per_device(): return (both[:, :K], both[:, K:])  1.32 us

profile of v9, /device:TPU:0, one launch (start us, length us, event | category | flops | bytes accessed | tf_op | source)
XLA Modules:
  0.0 56.6 jit_solution(11219545795301325457)
XLA Ops:
  0.6 54.7 %shard_map.104 = f32[4,1024]{1,0:T(4,128)} custom-call(bf16[16,8,48,512]{3,2,1,0:T(8,128)(2,1)} %v_hbm.1, f32[2,16,8,48]{3,2,1,0:T(8,128)} %mat.1, bf16[240,240]{1,0:T(8,128)(2,1)} %constant.14.clone.tz_ref, f32[128,256]{1,0:T(8,128)} %constant.15.clone.sel_ref, f32[128,256]{1,0:T(8,128)} %constant.16.clone.txy_ref, bf16[128,256]{1,0:T(8,128)(2,1)} %constant.17.clone.t2_ref, ...), custom_call_target="tpu_custom_call" | custom-call | tf_op jit(solution)/shard_map/pallas_call | solution.py:601
  55.3 1.3 %fusion = (f32[4,512]{1,0:T(4,128)}, f32[4,512]{1,0:T(4,128)}) fusion(f32[4,1024]{1,0:T(4,128)} %shard_map.104), kind=kLoop, calls=%fused_computation | loop fusion | bytes 32768 | tf_op jit(solution)/shard_map/slice | solution.py:638

commit v10 on v9

--- a/solution.py
+++ b/solution.py
@@ -433,7 +433,6 @@
             cell_pair(x + 2 * half, (0, 1, 2, 3) if half == 0 else (2, 3, 0, 1), half)
             for n in range(2):
                 wait_rows(x + 2 * half + 3 + n)
-            for n in range(2):
                 plane_stage(x + 2 * half + 4 + n, 2 * half + n)
 
         @pl.when(t == 0)

time: 56.8 us -> 57 us (level)
  no operation moved by 1% of the time
where the time goes in v10:
time: 57 us; the launch traced here: 56.8 us
  Pallas kernels  54.9 us (96%)
  local copies, waits for them, and re-layouts  1.32 us (2%)
  between operations  0.64 us (1%)
    pallas_call x1, Pallas kernels, local_products(): pl.pallas_call(local_kernel, out_shape=jax.ShapeDtypeStruct((4, 2 * K), F...  54.9 us
    slice x1, local copies, waits for them, and re-layouts, per_device(): return (both[:, :K], both[:, K:])  1.32 us

profile of v10, /device:TPU:0, one launch (start us, length us, event | category | flops | bytes accessed | tf_op | source)
XLA Modules:
  0.0 56.8 jit_solution(15831569546971374227)
XLA Ops:
  0.6 54.9 %shard_map.104 = f32[4,1024]{1,0:T(4,128)} custom-call(bf16[16,8,48,512]{3,2,1,0:T(8,128)(2,1)} %v_hbm.1, f32[2,16,8,48]{3,2,1,0:T(8,128)} %mat.1, bf16[240,240]{1,0:T(8,128)(2,1)} %constant.14.clone.tz_ref, f32[128,256]{1,0:T(8,128)} %constant.15.clone.sel_ref, f32[128,256]{1,0:T(8,128)} %constant.16.clone.txy_ref, bf16[128,256]{1,0:T(8,128)(2,1)} %constant.17.clone.t2_ref, ...), custom_call_target="tpu_custom_call" | custom-call | tf_op jit(solution)/shard_map/pallas_call | solution.py:600
  55.5 1.3 %fusion = (f32[4,512]{1,0:T(4,128)}, f32[4,512]{1,0:T(4,128)}) fusion(f32[4,1024]{1,0:T(4,128)} %shard_map.104), kind=kLoop, calls=%fused_computation | loop fusion | bytes 32768 | tf_op jit(solution)/shard_map/slice | solution.py:637
